TPU v7x, 16 devices: a whole 2x2x2 slice. The times are simulated.
16 devices in a mesh: tp: 4 (over z, y), ep: 4 (over x, core).
Axes of the slice: x: 2, y: 2, z: 2, core: 2. Of those that a mesh axis runs over, the one named last changes fastest.
Arguments:
- x: bfloat16 [1024, 1536], P(('ep', 'tp'))
- grad_y: bfloat16 [1024, 1536], P(('ep', 'tp'))
- w_router: bfloat16 [1536, 64], replicated
- w_gate: bfloat16 [64, 1536, 512], P('ep', None, 'tp')
- w_up: bfloat16 [64, 1536, 512], P('ep', None, 'tp')
- w_down: bfloat16 [64, 512, 1536], P('ep', 'tp')
- ws_gate: bfloat16 [1536, 1024], P(None, 'tp')
- ws_up: bfloat16 [1536, 1024], P(None, 'tp')
- ws_down: bfloat16 [1024, 1536], P('tp')
- topk_idx: int32 [1024, 6], P(('ep', 'tp'))
Outputs:
- output 1: bfloat16 [1024, 1536], P(('ep', 'tp'))
- output 2: bfloat16 [1024, 1536], P(('ep', 'tp'))
- output 3: float32 [1536, 64], replicated
- output 4: float32 [64, 1536, 512], P('ep', None, 'tp')
- output 5: float32 [64, 1536, 512], P('ep', None, 'tp')
- output 6: float32 [64, 512, 1536], P('ep', 'tp')
- output 7: float32 [1536, 1024], P(None, 'tp')
- output 8: float32 [1536, 1024], P(None, 'tp')
- output 9: float32 [1024, 1536], P('tp')
All inputs are finite; a program needn't handle non-finite values.
Results may differ from a plain program's by a relative error of at most 0.0143696.
Values are sent between devices in bfloat16 or wider.
A program may use at most 1 GiB of HBM per device.

v0:
```python
import jax
import jax.numpy as jnp
from jax import lax
from jax.sharding import PartitionSpec as P

GATE_SCALE = 16.0


def capacity(tok_rows, top_k, experts, ep_size):
    groups = top_k // 2
    most = groups * tok_rows // (2 * ep_size) + min(groups, ep_size // 2) * tok_rows // ep_size
    per_group = experts // ep_size
    return (2 * most + per_group - 1) // per_group


def slot_maps(topk_idx, route_gates, experts, capacity_rows):
    tok_rows = topk_idx.shape[0]
    n_slots = experts * capacity_rows
    hit_count = jnp.sum(jax.nn.one_hot(topk_idx, experts, dtype=jnp.int32), axis=1)
    slot_rank = jnp.cumsum(hit_count, axis=0) - hit_count
    slot_of = topk_idx * capacity_rows + jnp.take_along_axis(slot_rank, topk_idx, axis=1)
    flat_slot = slot_of.reshape(-1)
    token_ids = jnp.broadcast_to(jnp.arange(tok_rows, dtype=jnp.int32)[:, None], slot_of.shape).reshape(-1)
    slot_owner = jax.ops.segment_sum(token_ids - tok_rows, flat_slot, num_segments=n_slots) + tok_rows
    gate_slot = jax.ops.segment_sum(route_gates.reshape(-1), flat_slot, num_segments=n_slots)
    return slot_of, slot_owner, gate_slot


def swiglu_act(gate_pre, up_pre):
    return jax.nn.silu(gate_pre) * up_pre


def solution(mesh):
    tp_size = mesh.shape['tp']
    ep_size = mesh.shape['ep']

    def device_step(x, grad_y, w_router, w_gate, w_up, w_down, ws_gate, ws_up, ws_down, topk_idx):
        tok_rows, model_dim = x.shape
        top_k = topk_idx.shape[1]
        experts = w_router.shape[1]
        local_exp = w_gate.shape[0]
        capacity_rows = capacity(tok_rows, top_k, experts, ep_size)
        n_slots = experts * capacity_rows
        router_probs = jax.nn.softmax(jnp.dot(x, w_router, preferred_element_type=jnp.float32), axis=-1)
        route_gates = GATE_SCALE * jnp.take_along_axis(router_probs, topk_idx, axis=1)
        slot_of, slot_owner, gate_slot = slot_maps(topk_idx, route_gates, experts, capacity_rows)
        send_rows = jnp.take(x, slot_owner, axis=0, mode='fill', fill_value=0).reshape(ep_size, local_exp, capacity_rows, model_dim)
        recv_rows = lax.all_to_all(send_rows, 'ep', 0, 0)
        expert_rows = lax.all_gather(recv_rows, 'tp', axis=0)
        gate_pre = jnp.einsum('tsecd,edf->tsecf', expert_rows, w_gate, preferred_element_type=jnp.float32).astype(jnp.bfloat16)
        up_pre = jnp.einsum('tsecd,edf->tsecf', expert_rows, w_up, preferred_element_type=jnp.float32).astype(jnp.bfloat16)
        hidden_act = swiglu_act(gate_pre.astype(jnp.float32), up_pre.astype(jnp.float32)).astype(jnp.bfloat16)
        part_out = jnp.einsum('tsecf,efd->tsecd', hidden_act, w_down, preferred_element_type=jnp.float32)
        own_out = lax.psum_scatter(part_out, 'tp', scatter_dimension=0).astype(jnp.bfloat16)
        back_rows = lax.all_to_all(own_out, 'ep', 0, 0).reshape(n_slots, model_dim)
        picked = jnp.take(back_rows, slot_of, axis=0)
        routed = jnp.einsum('tk,tkd->td', route_gates, picked, preferred_element_type=jnp.float32)
        x_group = lax.all_gather(x, 'tp', axis=0, tiled=True)
        sg_pre = jnp.dot(x_group, ws_gate, preferred_element_type=jnp.float32).astype(jnp.bfloat16)
        su_pre = jnp.dot(x_group, ws_up, preferred_element_type=jnp.float32).astype(jnp.bfloat16)
        s_hidden = swiglu_act(sg_pre.astype(jnp.float32), su_pre.astype(jnp.float32)).astype(jnp.bfloat16)
        shared = lax.psum_scatter(jnp.dot(s_hidden, ws_down, preferred_element_type=jnp.float32), 'tp', scatter_dimension=0, tiled=True)
        y_out = (shared + routed).astype(jnp.bfloat16)

        d_gates = jnp.einsum('td,tkd->tk', grad_y, picked, preferred_element_type=jnp.float32)
        d_out = (jnp.take(grad_y, slot_owner, axis=0, mode='fill', fill_value=0) * gate_slot[:, None]).astype(jnp.bfloat16)
        d_recv = lax.all_to_all(d_out.reshape(ep_size, local_exp, capacity_rows, model_dim), 'ep', 0, 0)
        d_rows_in = lax.all_gather(d_recv, 'tp', axis=0)
        d_hidden = jnp.einsum('tsecd,efd->tsecf', d_rows_in, w_down, preferred_element_type=jnp.float32).astype(jnp.bfloat16)
        d_w_down = jnp.einsum('tsecf,tsecd->efd', hidden_act, d_rows_in, preferred_element_type=jnp.float32)
        act_out, act_vjp = jax.vjp(swiglu_act, gate_pre.astype(jnp.float32), up_pre.astype(jnp.float32))
        d_gate_pre, d_up_pre = act_vjp(d_hidden.astype(jnp.float32))
        d_gate_pre = d_gate_pre.astype(jnp.bfloat16)
        d_up_pre = d_up_pre.astype(jnp.bfloat16)
        d_w_gate = jnp.einsum('tsecd,tsecf->edf', expert_rows, d_gate_pre, preferred_element_type=jnp.float32)
        d_w_up = jnp.einsum('tsecd,tsecf->edf', expert_rows, d_up_pre, preferred_element_type=jnp.float32)
        d_rows_part = jnp.einsum('tsecf,edf->tsecd', d_gate_pre, w_gate, preferred_element_type=jnp.float32) + jnp.einsum('tsecf,edf->tsecd', d_up_pre, w_up, preferred_element_type=jnp.float32)
        d_own = lax.psum_scatter(d_rows_part, 'tp', scatter_dimension=0).astype(jnp.bfloat16)
        d_back = lax.all_to_all(d_own, 'ep', 0, 0).reshape(n_slots, model_dim)
        dx_routed = jnp.sum(jnp.take(d_back, slot_of, axis=0), axis=1, dtype=jnp.float32)
        d_scores = GATE_SCALE * jnp.einsum('tk,tke->te', d_gates, jax.nn.one_hot(topk_idx, experts, dtype=jnp.float32))
        d_logits = router_probs * (d_scores - jnp.sum(router_probs * d_scores, axis=-1, keepdims=True))
        d_router = lax.psum(jnp.einsum('td,te->de', x, d_logits, preferred_element_type=jnp.float32), ('tp', 'ep'))
        dx_router = jnp.einsum('te,de->td', d_logits, w_router, preferred_element_type=jnp.float32)
        dy_group = lax.all_gather(grad_y, 'tp', axis=0, tiled=True)
        ds_hidden = jnp.einsum('td,fd->tf', dy_group, ws_down, preferred_element_type=jnp.float32).astype(jnp.bfloat16)
        ds_down = lax.psum(jnp.einsum('tf,td->fd', s_hidden, dy_group, preferred_element_type=jnp.float32), 'ep')
        s_out, s_vjp = jax.vjp(swiglu_act, sg_pre.astype(jnp.float32), su_pre.astype(jnp.float32))
        dsg_pre, dsu_pre = s_vjp(ds_hidden.astype(jnp.float32))
        dsg_pre = dsg_pre.astype(jnp.bfloat16)
        dsu_pre = dsu_pre.astype(jnp.bfloat16)
        ds_gate = lax.psum(jnp.einsum('td,tf->df', x_group, dsg_pre, preferred_element_type=jnp.float32), 'ep')
        ds_up = lax.psum(jnp.einsum('td,tf->df', x_group, dsu_pre, preferred_element_type=jnp.float32), 'ep')
        dx_part = jnp.einsum('tf,df->td', dsg_pre, ws_gate, preferred_element_type=jnp.float32) + jnp.einsum('tf,df->td', dsu_pre, ws_up, preferred_element_type=jnp.float32)
        dx_shared = lax.psum_scatter(dx_part, 'tp', scatter_dimension=0, tiled=True)
        dx_out = (dx_router + dx_shared + dx_routed).astype(jnp.bfloat16)
        return y_out, dx_out, d_router, d_w_gate, d_w_up, d_w_down, ds_gate, ds_up, ds_down

    tok_spec = P(('ep', 'tp'), None)
    in_specs = (tok_spec, tok_spec, P(None, None), P('ep', None, 'tp'), P('ep', None, 'tp'), P('ep', 'tp', None), P(None, 'tp'), P(None, 'tp'), P('tp', None), tok_spec)
    out_specs = (tok_spec, tok_spec, P(None, None), P('ep', None, 'tp'), P('ep', None, 'tp'), P('ep', 'tp', None), P(None, 'tp'), P(None, 'tp'), P('tp', None))
    return jax.shard_map(device_step, mesh=mesh, in_specs=in_specs, out_specs=out_specs, check_vma=False)
```

profile of v0, /device:TPU:0, one launch (start us, length us, event | category | flops | bytes accessed | tf_op | source)
XLA Modules:
  0.0 657.8 jit_solution(8719364705998531269)
XLA Ops:
  23.8 22.2 %all_to_all.20 = bf16[4,16,7,1536]{3,1,2,0:T(8,128)(2,1)} all-to-all(bf16[4,16,7,1536]{3,1,2,0:T(8,128)(2,1)S(1)} %copy.104), channel_id=1, replica_groups=mesh['tp'=4,'ep'=4] {'ep'}, dimensions={0} | all-to-all | bytes 2752512 | tf_op jit(solution)/shard_map/all_to_all | solution.py:48
  46.5 59.9 %all-gather.5.cloned.1.call-done = bf16[16,16,7,1536]{3,1,2,0:T(8,128)(2,1)} async-done(((bf16[4,16,7,1536]{3,1,2,0:T(8,128)(2,1)}), bf16[16,16,7,1536]{3,1,2,0:T(8,128)(2,1)}) %all-gather.5.cloned.1.call-update) | async-done | bytes 5505040 | tf_op jit(solution)/shard_map/all_gather | solution.py:49
  106.4 5.8 copy.105
  112.2 5.9 fusion.32
  118.2 7.3 %multiply_convert_fusion.2 = (bf16[4,4,16,7,128]{4,3,1,0,2:T(8,128)(2,1)S(1)}, f32[4,4,16,7,128]{4,3,1,0,2:T(8,128)}) fusion(f32[4,4,16,7,128]{4,3,1,0,2:T(8,128)S(1)} %fusion.32, bf16[4,4,16,7,1536]{4,3,1,0,2:T(8,128)(2,1)S(1)} %bitcast.140, bf16[16,1536,128]{2,1,0:T(8,128)(2,1)} %param.18), kind=kOutput, calls=%fused_computation.63 | convolution fusion | flops 706478080 | bytes 14090240 | tf_op jit(solution)/shard_map/tsecd,edf->tsecf/dot_general | solution.py:51
  125.5 6.4 convolution_bitcast_fusion.3
  131.8 17.5 %copy.106 = f32[4,4,16,7,1536]{4,2,3,1,0:T(8,128)} copy(f32[4,4,16,7,1536]{4,3,1,0,2:T(8,128)} %convolution_bitcast_fusion.3) | data formatting | bytes 22020096 | tf_op jit(solution)/shard_map/tsecf,efd->tsecd/transpose | solution.py:53
  149.4 103.9 %reduce-scatter.13.cloned.1.call-done = f32[1,4,16,7,1536]{4,2,3,1,0:T(8,128)} async-done(((f32[4,4,16,7,1536]{4,2,3,1,0:T(8,128)}), f32[1,4,16,7,1536]{4,2,3,1,0:T(8,128)}) %reduce-scatter.13.cloned.1.call-update) | async-done | bytes 2752528
  264.0 13.8 %all-to-all-done.1 = bf16[4,16,7,1536]{3,1,2,0:T(8,128)(2,1)S(1)} async-done(((bf16[4,16,7,1536]{3,1,2,0:T(8,128)(2,1)}), bf16[4,16,7,1536]{3,1,2,0:T(8,128)(2,1)S(1)}, u32[]{:S(2)}, u32[]{:S(2)}) %all-to-all-start.1) | async-done | bytes 1376288 | tf_op jit(solution)/shard_map/all_to_all | solution.py:55
  300.3 21.0 %all_to_all.21 = bf16[4,16,7,1536]{3,1,2,0:T(8,128)(2,1)} all-to-all(bf16[4,16,7,1536]{3,1,2,0:T(8,128)(2,1)S(1)} %copy.111), channel_id=1, replica_groups=mesh['tp'=4,'ep'=4] {'ep'}, dimensions={0} | all-to-all | bytes 2752512 | tf_op jit(solution)/shard_map/all_to_all | solution.py:67
  321.3 15.9 %all_gather.18 = bf16[256,1536]{1,0:T(8,128)(2,1)S(1)} all-gather(bf16[64,1536]{1,0:T(8,128)(2,1)S(1)} %copy-done.2), channel_id=1, replica_groups=mesh['tp'=4,'ep'=4] {'tp'}, dimensions={0}, use_global_device_ids=true | all-gather | bytes 983040 | tf_op jit(solution)/shard_map/all_gather | solution.py:58
  337.3 16.3 %all_gather.21 = bf16[256,1536]{1,0:T(8,128)(2,1)S(1)} all-gather(bf16[64,1536]{1,0:T(8,128)(2,1)S(1)} %copy-done.3), channel_id=1, replica_groups=mesh['tp'=4,'ep'=4] {'tp'}, dimensions={0}, use_global_device_ids=true | all-gather | bytes 983040 | tf_op jit(solution)/shard_map/all_gather | solution.py:85
  362.6 25.1 %all-gather.7.cloned.1.call-done = bf16[16,16,7,1536]{3,1,2,0:T(8,128)(2,1)} async-done(((bf16[4,16,7,1536]{3,1,2,0:T(8,128)(2,1)}), bf16[16,16,7,1536]{3,1,2,0:T(8,128)(2,1)}) %all-gather.7.cloned.1.call-update) | async-done | bytes 5505040 | tf_op jit(solution)/shard_map/all_gather | solution.py:68
  387.7 8.5 %copy.112 = bf16[16,16,7,1536]{3,2,0,1:T(8,128)(2,1)} copy(bf16[16,16,7,1536]{3,1,2,0:T(8,128)(2,1)} %all-gather.7.cloned.1.call-done) | data formatting | bytes 11010048 | tf_op jit(solution)/shard_map/all_gather | solution.py:68
  396.2 9.3 %multiply_convert_fusion.1 = (bf16[4,4,16,7,128]{4,3,1,0,2:T(8,128)(2,1)}, bf16[4,4,16,7,128]{4,3,1,0,2:T(8,128)(2,1)S(1)}) fusion(f32[4,4,16,7,128]{4,3,1,0,2:T(8,128)} %copy-done.5, f32[4,4,16,7,128]{4,3,1,0,2:T(8,128)} %get-tuple-element.69, bf16[4,4,16,7,1536]{4,3,1,0,2:T(8,128)(2,1)} %bitcast.143, bf16[16,128,1536]{2,1,0:T(8,128)(2,1)} %param.19), kind=kOutput, calls=%fused_computation.62 | convolution fusion | flops 708313088 | bytes 14548992 | tf_op jit(solution)/shard_map/tsecd,efd->tsecf/dot_general | solution.py:69
  405.5 6.6 %fusion.4 = f32[16,4,4,7,1536]{4,3,2,1,0:T(8,128)} fusion(bf16[4,4,16,7,128]{4,3,1,0,2:T(8,128)(2,1)S(1)} %get-tuple-element.64, bf16[16,1536,128]{2,1,0:T(8,128)(2,1)S(1)} %bitcast.138), kind=kOutput, calls=%fused_computation.17 | convolution fusion | flops 704643072 | bytes 17760256 | tf_op jit(solution)/shard_map/tsecf,edf->tsecd/dot_general | solution.py:77
  412.1 13.1 %add_bitcast_fusion = f32[4,4,16,7,1536]{4,3,1,0,2:T(8,128)} fusion(f32[16,4,4,7,1536]{4,3,2,1,0:T(8,128)} %fusion.4, bf16[4,4,16,7,128]{4,3,1,0,2:T(8,128)(2,1)S(1)} %copy-done.18, bf16[16,1536,128]{2,1,0:T(8,128)(2,1)} %param.18), kind=kOutput, calls=%fused_computation.8 | convolution fusion | flops 707395584 | bytes 28770304 | tf_op jit(solution)/shard_map/tsecf,edf->tsecd/dot_general | solution.py:77
  425.2 17.4 %copy.113 = f32[4,4,16,7,1536]{4,2,3,1,0:T(8,128)} copy(f32[4,4,16,7,1536]{4,3,1,0,2:T(8,128)} %add_bitcast_fusion) | data formatting | bytes 22020096 | tf_op jit(solution)/shard_map/add | solution.py:77
  445.8 4.0 all-reduce.8.cloned.1.call-done
  460.9 16.6 %convolution_bitcast_fusion.1 = f32[16,1536,128]{2,1,0:T(8,128)} fusion(bf16[4,4,16,7,1536]{4,2,3,1,0:T(8,128)(2,1)} %bitcast.144, bf16[4,4,16,7,128]{4,3,1,0,2:T(8,128)(2,1)S(1)} %copy-done.19), kind=kOutput, calls=%fused_computation.10 | convolution fusion | flops 704643072 | bytes 18546688 | tf_op jit(solution)/shard_map/tsecd,tsecf->edf/dot_general | solution.py:76
  477.5 13.3 %convolution_bitcast_fusion.2 = f32[16,1536,128]{2,1,0:T(8,128)} fusion(bf16[4,4,16,7,1536]{4,2,3,1,0:T(8,128)(2,1)S(1)} %bitcast.147, bf16[4,4,16,7,128]{4,3,1,0,2:T(8,128)(2,1)S(1)} %copy-done.9), kind=kOutput, calls=%fused_computation.11 | convolution fusion | flops 704643072 | bytes 18546688 | tf_op jit(solution)/shard_map/tsecd,tsecf->edf/dot_general | solution.py:75
  490.7 55.9 %reduce-scatter.15.cloned.1.call-done = f32[1,4,16,7,1536]{4,2,3,1,0:T(8,128)} async-done(((f32[4,4,16,7,1536]{4,2,3,1,0:T(8,128)}), f32[1,4,16,7,1536]{4,2,3,1,0:T(8,128)}) %reduce-scatter.15.cloned.1.call-update) | async-done | bytes 2752528
  553.6 17.7 %convolution_bitcast_fusion = f32[16,128,1536]{2,1,0:T(8,128)} fusion(bf16[4,4,16,7,1536]{4,2,3,1,0:T(8,128)(2,1)} %bitcast.148, bf16[4,4,16,7,128]{4,3,1,0,2:T(8,128)(2,1)S(1)} %copy-done.15), kind=kOutput, calls=%fused_computation.9 | convolution fusion | flops 704643072 | bytes 18546688 | tf_op jit(solution)/shard_map/tsecf,tsecd->efd/dot_general | solution.py:70
  584.0 62.9 %all-reduce.6.cloned.1.call-done = f32[1536,64]{0,1:T(8,128)} async-done(((f32[1536,64]{0,1:T(8,128)}), f32[1536,64]{0,1:T(8,128)}) %all-reduce.6.cloned.1.call-update) | async-done | bytes 393232 | tf_op jit(solution)/shard_map/psum | solution.py:83
  (155 shorter events, 95.1 us)
Async XLA Ops:
  8.0 347.5 %copy-start = (bf16[256,1536]{1,0:T(8,128)(2,1)S(1)}, bf16[256,1536]{1,0:T(8,128)(2,1)}, u32[]{:S(2)}) copy-start(bf16[256,1536]{1,0:T(8,128)(2,1)} %param.22) | copy-start | bytes 2359300
  8.0 98.4 %all-gather.5.cloned.1.call-start = ((), (), s32[]{:S(2)}) async-start(), calls=%async_computation.11 | async-start | bytes 6881280 | tf_op jit(solution)/shard_map/all_gather | solution.py:49
  46.0 207.3 %reduce-scatter.13.cloned.1.call-start = ((), (), s32[]{:S(2)}) async-start(), calls=%async_computation.13 | async-start | bytes 13762560
  106.4 19.0 %slice-start.2 = ((s8[6291456]{0:T(1024)(128)(4,1)}), s8[4194304]{0:T(1024)(128)(4,1)S(1)}, s32[]{:S(2)}) async-start(s8[6291456]{0:T(1024)(128)(4,1)} %bitcast.141), calls=%async_computation.18 | async-start | bytes 8388608
  112.2 13.2 %slice-start.3 = ((s8[6291456]{0:T(1024)(128)(4,1)}), s8[2097152]{0:T(1024)(128)(4,1)S(1)}, s32[]{:S(2)}) async-start(s8[6291456]{0:T(1024)(128)(4,1)} %bitcast.141), calls=%async_computation.19 | async-start | bytes 4194304
  118.2 7.3 %copy-start.5 = (f32[4,4,16,7,128]{4,3,1,0,2:T(8,128)}, f32[4,4,16,7,128]{4,3,1,0,2:T(8,128)S(1)}, u32[]{:S(2)}) copy-start(f32[4,4,16,7,128]{4,3,1,0,2:T(8,128)S(1)} %fusion.32) | copy-start | bytes 2752516
  256.3 21.4 %all-to-all-start.1 = ((bf16[4,16,7,1536]{3,1,2,0:T(8,128)(2,1)}), bf16[4,16,7,1536]{3,1,2,0:T(8,128)(2,1)S(1)}, u32[]{:S(2)}, u32[]{:S(2)}) async-start(bf16[4,16,7,1536]{3,1,2,0:T(8,128)(2,1)} %convert_bitcast_fusion.1), calls=%async_computation.2 | async-start | bytes 2752512 | tf_op jit(solution)/shard_map/all_to_all | solution.py:55
  260.0 127.7 %all-gather.7.cloned.1.call-start = ((), (), s32[]{:S(2)}) async-start(), calls=%async_computation.12 | async-start | bytes 6881280 | tf_op jit(solution)/shard_map/all_gather | solution.py:68
  263.6 18.5 %copy-start.12 = (s32[1024]{0:T(1024)}, s32[1024]{0:T(1024)S(1)}, u32[]{:S(2)}) copy-start(s32[1024]{0:T(1024)S(1)} %pad_clamp_fusion) | copy-start | bytes 12292
  288.6 7.4 %copy-start.4 = (bf16[448,1536]{1,0:T(8,128)(2,1)S(1)}, bf16[448,1536]{1,0:T(8,128)(2,1)}, u32[]{:S(2)}) copy-start(bf16[448,1536]{1,0:T(8,128)(2,1)} %gather_fusion.4) | copy-start | bytes 4128772
  321.3 128.5 %all-reduce.8.cloned.1.call-start = ((), (), s32[]{:S(2)}) async-start(), calls=%async_computation.15 | async-start | bytes 9437184 | tf_op jit(solution)/shard_map/psum | solution.py:92
  337.3 17.8 %copy-start.6 = (bf16[1536,256]{1,0:T(8,128)(2,1)S(1)}, bf16[1536,256]{1,0:T(8,128)(2,1)}, u32[]{:S(2)}) copy-start(bf16[1536,256]{1,0:T(8,128)(2,1)} %param.20) | copy-start | bytes 2359300
  360.6 98.6 %reduce-scatter.9.cloned.1.call-start = ((), (), s32[]{:S(2)}) async-start(), calls=%async_computation.8 | async-start | bytes 1966080 | tf_op jit(solution)/shard_map/reduce_scatter | solution.py:62
  362.2 184.5 %reduce-scatter.15.cloned.1.call-start = ((), (), s32[]{:S(2)}) async-start(), calls=%async_computation.14 | async-start | bytes 13762560
  387.7 17.8 %slice-start = ((s8[6291456]{0:T(1024)(128)(4,1)}), s8[4194304]{0:T(1024)(128)(4,1)S(1)}, s32[]{:S(2)}) async-start(s8[6291456]{0:T(1024)(128)(4,1)} %bitcast.137), calls=%async_computation.16 | async-start | bytes 8388608
  396.2 9.3 %slice-start.1 = ((s8[6291456]{0:T(1024)(128)(4,1)}), s8[2097152]{0:T(1024)(128)(4,1)S(1)}, s32[]{:S(2)}) async-start(s8[6291456]{0:T(1024)(128)(4,1)} %bitcast.137), calls=%async_computation.17 | async-start | bytes 4194304
  405.5 6.7 %copy-start.8 = (bf16[4,4,16,7,128]{4,3,1,0,2:T(8,128)(2,1)}, bf16[4,4,16,7,128]{4,3,1,0,2:T(8,128)(2,1)S(1)}, u32[]{:S(2)}) copy-start(bf16[4,4,16,7,128]{4,3,1,0,2:T(8,128)(2,1)S(1)} %get-tuple-element.64) | copy-start | bytes 1376260
  442.7 139.3 %reduce-scatter.11.cloned.1.call-start = ((), (), s32[]{:S(2)}) async-start(), calls=%async_computation.9 | async-start | bytes 1966080 | tf_op jit(solution)/shard_map/reduce_scatter | solution.py:95
  445.6 201.4 %all-reduce.6.cloned.1.call-start = ((), (), s32[]{:S(2)}) async-start(), calls=%async_computation.10 | async-start | bytes 786432 | tf_op jit(solution)/shard_map/psum | solution.py:83
  452.8 24.6 %slice-start.4 = ((s8[5505024]{0:T(1024)(128)(4,1)}), s8[1310720]{0:T(1024)(128)(4,1)S(1)}, s32[]{:S(2)}) async-start(s8[5505024]{0:T(1024)(128)(4,1)} %bitcast.145), calls=%async_computation.20 | async-start | bytes 2621440
  460.9 16.6 %slice-start.5 = ((s8[5505024]{0:T(1024)(128)(4,1)}), s8[4194304]{0:T(1024)(128)(4,1)S(1)}, s32[]{:S(2)}) async-start(s8[5505024]{0:T(1024)(128)(4,1)} %bitcast.145), calls=%async_computation.21 | async-start | bytes 8388608
  460.9 16.6 %copy-start.9 = (bf16[4,4,16,7,128]{4,3,1,0,2:T(8,128)(2,1)S(1)}, bf16[4,4,16,7,128]{4,3,1,0,2:T(8,128)(2,1)}, u32[]{:S(2)}) copy-start(bf16[4,4,16,7,128]{4,3,1,0,2:T(8,128)(2,1)} %copy-done.8) | copy-start | bytes 1376260
  549.7 21.6 %all-to-all-start.3 = ((bf16[4,16,7,1536]{3,1,2,0:T(8,128)(2,1)}), bf16[4,16,7,1536]{3,1,2,0:T(8,128)(2,1)S(1)}, u32[]{:S(2)}, u32[]{:S(2)}) async-start(bf16[4,16,7,1536]{3,1,2,0:T(8,128)(2,1)} %convert_bitcast_fusion), calls=%async_computation.5 | async-start | bytes 2752512 | tf_op jit(solution)/shard_map/all_to_all | solution.py:79
  582.0 66.8 %copy-start.10 = (f32[256,1536]{1,0:T(8,128)S(1)}, f32[256,1536]{1,0:T(8,128)}, u32[]{:S(2)}) copy-start(f32[256,1536]{1,0:T(8,128)} %get-tuple-element.80) | copy-start | bytes 4718596
  (15 other events, 49.2 us)
Sparse Core Ops, SparseCore 0:
  46.1 60.2 all-gather.4
  149.5 103.7 reduce-scatter.12
  321.4 66.2 all-gather.6
  391.1 27.2 reduce-scatter.8
  442.8 103.7 reduce-scatter.14
  549.4 27.2 reduce-scatter.10
  581.5 65.3 all-reduce.5
Sparse Core Ops, SparseCore 1:
  360.7 89.1 all-reduce.7
where the time goes:
time: 663 us; the launch traced here: 658 us
  waiting for transfers between devices  326 us (49%)
  matrix products  113 us (17%)
  local copies, waits for them, and re-layouts  96.3 us (15%)
  blocking collectives  75.5 us (11%)
  other arithmetic  21.5 us (3%)
  between operations  16.6 us (3%)
  starting transfers between devices  9.23 us (1%)
    unnamed x10, waiting for transfers between devices  160 us
    psum x1, waiting for transfers between devices, device_step(): lax.psum(jnp.einsum('td,te->de', x, d_logits, preferred_element_type=jnp....  62.9 us
    all_gather x1, waiting for transfers between devices, device_step(): expert_rows = lax.all_gather(recv_rows, 'tp', axis=0)  59.9 us
    all_gather x1, waiting for transfers between devices, device_step(): d_rows_in = lax.all_gather(d_recv, 'tp', axis=0)  25.1 us
    all_to_all x1, blocking collectives, device_step(): recv_rows = lax.all_to_all(send_rows, 'ep', 0, 0)  22.2 us
    all_to_all x1, blocking collectives, device_step(): lax.all_to_all(d_out.reshape(ep_size, local_exp, capacity_rows, model_dim...  21 us
    dot_general x1, matrix products, device_step(): jnp.einsum('tsecf,tsecd->efd', hidden_act, d_rows_in, preferred_element_t...  17.7 us
    transpose x1, local copies, waits for them, and re-layouts, device_step(): jnp.einsum('tsecf,efd->tsecd', hidden_act, w_down, preferred_element_type...  17.5 us
  transfers between devices with their start and end apart: 10, of which 7 were waited for; matrix products, arithmetic and copies ran while one was open for 22% of the time, Pallas kernels for 0%

commit v1 on v0

v1 whole, which is shorter than its diff:
```python
import functools

import jax
import jax.numpy as jnp
from jax import lax
from jax.experimental import pallas as pl
from jax.experimental.pallas import tpu as pltpu
from jax.sharding import PartitionSpec as P

GATE_SCALE = 16.0
BF = jnp.bfloat16
F32 = jnp.float32
MESH = pl.DeviceIdType.MESH

D = 1536
EXPERTS = 64
TOP = 6
TOK = 64
TP = 4
EP = 4
NDEV = TP * EP
LOCAL = EXPERTS // EP
CAP = 7
STRIP = 8
ROWS = NDEV * STRIP
PAIR_ROWS = 2 * EP * CAP
STEPS = LOCAL // 2
SH_ROWS = 2 * TOK // STEPS
BLK = PAIR_ROWS + SH_ROWS

BIT_Y, BIT_Z, BIT_C, BIT_X = 1, 2, 4, 8


def flip(value, bit):
    return value + bit * (1 - 2 * ((value // bit) % 2))


def flip_mask(value, mask):
    for bit in (1, 2, 4, 8):
        if mask & bit:
            value = flip(value, bit)
    return value


def dot(a, b):
    return jnp.dot(a, b, preferred_element_type=F32)


def dot_nt(a, b):
    return lax.dot_general(a, b, (((1,), (1,)), ((), ())), preferred_element_type=F32)


def dot_tn(a, b):
    return lax.dot_general(a, b, (((0,), (0,)), ((), ())), preferred_element_type=F32)


def act_both(a, b, dh):
    sig = 1.0 / (1.0 + jnp.exp(-a))
    silu = a * sig
    h = (silu * b).astype(BF)
    db = (dh * silu).astype(BF)
    da = (dh * b * (sig * (1.0 + a * (1.0 - sig)))).astype(BF)
    return h, da, db


def gather_kernel(rows_ref, tab_ref, all_ref, tabs_ref, send_sem, recv_sem, local_sem):
    tp = lax.axis_index('tp')
    ep = lax.axis_index('ep')
    me = ep * TP + tp
    third = D // 3

    def peer(mask):
        return (flip_mask(tp, mask & 3), flip_mask(ep, mask >> 2))

    barrier = pltpu.get_barrier_semaphore()
    for mask in (BIT_X, BIT_Y, BIT_Z, BIT_C):
        pl.semaphore_signal(barrier, inc=1, device_id=peer(mask), device_id_type=MESH)
    pl.semaphore_wait(barrier, 4)

    orders = [(BIT_X, BIT_Y, BIT_Z), (BIT_Y, BIT_Z, BIT_X), (BIT_Z, BIT_X, BIT_Y), (BIT_X, BIT_Y, BIT_Z)]

    def view(part, block, own):
        if part == 3:
            return tab_ref if own else tabs_ref.at[block]
        cols = pl.ds(part * third, third)
        return rows_ref.at[:, cols] if own else all_ref.at[block, :, cols]

    def copy(part, k, mask):
        block = flip_mask(me, k)
        return pltpu.make_async_remote_copy(
            src_ref=view(part, block, k == 0), dst_ref=view(part, block, False),
            send_sem=send_sem.at[part, k ^ mask], recv_sem=recv_sem.at[part, k ^ mask],
            device_id=peer(mask), device_id_type=MESH)

    sent = []

    def send(part, k, mask):
        c = copy(part, k, mask)
        c.start()
        sent.append(c)

    def arrived(part, k):
        block = flip_mask(me, k)
        pltpu.make_async_remote_copy(
            src_ref=view(part, block, False), dst_ref=view(part, block, False),
            send_sem=send_sem.at[part, k], recv_sem=recv_sem.at[part, k],
            device_id=peer(BIT_C), device_id_type=MESH).wait_recv()

    parts = (3, 0, 1, 2)
    for step in range(3):
        for part in parts:
            send(part, 0, orders[part][step])
    for part in parts:
        send(part, 0, BIT_C)
    own_rows = pltpu.make_async_copy(rows_ref, all_ref.at[me], local_sem.at[0])
    own_tab = pltpu.make_async_copy(tab_ref, tabs_ref.at[me], local_sem.at[1])
    own_rows.start()
    own_tab.start()
    for part in parts:
        m1, m2, m3 = orders[part]
        arrived(part, m1)
        send(part, m1, m2)
        send(part, m1, m3)
        send(part, m1, BIT_C)
    for part in parts:
        m1, m2, m3 = orders[part]
        arrived(part, m2)
        send(part, m2, m3)
        send(part, m2, BIT_C)
    for part in parts:
        m1, m2, m3 = orders[part]
        arrived(part, m1 ^ m2)
        send(part, m1 ^ m2, m3)
        send(part, m1 ^ m2, BIT_C)
    for extra in range(4):
        for part in parts:
            m1, m2, m3 = orders[part]
            k = (m3, m1 ^ m3, m2 ^ m3, m1 ^ m2 ^ m3)[extra]
            arrived(part, k)
            send(part, k, BIT_C)
    for part in parts:
        for k in range(16):
            if k & BIT_C:
                arrived(part, k)
    own_rows.wait()
    own_tab.wait()
    for c in sent:
        c.wait_send()


def gather_rows(rows, tab):
    vmem = pl.BlockSpec(memory_space=pltpu.VMEM)
    return pl.pallas_call(
        gather_kernel,
        name='gather_rows',
        out_shape=(jax.ShapeDtypeStruct((NDEV,) + rows.shape, rows.dtype), jax.ShapeDtypeStruct((NDEV,) + tab.shape, tab.dtype)),
        in_specs=[vmem, vmem],
        out_specs=(vmem, vmem),
        scratch_shapes=[pltpu.SemaphoreType.DMA((4, 16)), pltpu.SemaphoreType.DMA((4, 16)), pltpu.SemaphoreType.DMA((2,))],
        compiler_params=pltpu.CompilerParams(collective_id=0, has_side_effects=True, vmem_limit_bytes=40 << 20),
        cost_estimate=pl.CostEstimate(flops=40_000_000_000, bytes_accessed=7_000_000, transcendentals=0),
    )(rows, tab)


def main_kernel(g_ref, all_ref, slot_ref, wr_ref, wsg_ref, wsu_ref, wsd_ref, perm_ref, wg_ref, wu_ref, wd_ref,
                part_ref, h_ref, dab_ref, xe_hbm, de_hbm, xe, de, sh, sems):
    step = pl.program_id(0)
    g = g_ref[0]
    third = D // 3
    xe_copy = pltpu.make_async_copy(xe, xe_hbm, sems.at[0])
    de_copy = pltpu.make_async_copy(de, de_hbm, sems.at[1])

    @pl.when(step == 0)
    def _():
        n_rows = LOCAL * EP * STRIP
        lane = lax.broadcasted_iota(jnp.int32, (n_rows, EP * TOK), 1)
        wr = wr_ref[...]
        row_expert = g * LOCAL + lax.broadcasted_iota(jnp.int32, (n_rows, 3 * EXPERTS), 0) // (EP * STRIP)
        wanted = lax.broadcasted_iota(jnp.int32, (n_rows, 3 * EXPERTS), 1) % EXPERTS == row_expert
        for j in range(TP):
            pick = jnp.where(slot_ref[j] == lane, 1.0, 0.0).astype(BF)
            x_j = jnp.concatenate([all_ref[s * TP + j, :TOK, :] for s in range(EP)], axis=0)
            logits = dot(x_j, wr)
            top = jnp.max(logits, axis=-1, keepdims=True)
            ex = jnp.exp(logits - top)
            probs = ex / jnp.sum(ex, axis=-1, keepdims=True)
            hi = probs.astype(BF)
            rest = probs - hi.astype(F32)
            mid = rest.astype(BF)
            low = (rest - mid.astype(F32)).astype(BF)
            sel = dot(pick, jnp.concatenate([hi, mid, low], axis=1))
            gate = GATE_SCALE * jnp.sum(jnp.where(wanted, sel, 0.0), axis=1, keepdims=True)
            for n in range(3):
                cols = slice(n * third, (n + 1) * third)
                got = dot(pick, x_j[:, cols]).astype(BF)
                xe[:, EP * STRIP * j:EP * STRIP * (j + 1), cols] = got.reshape(LOCAL, EP * STRIP, third)
                gy_j = jnp.concatenate([all_ref[s * TP + j, TOK:, cols] for s in range(EP)], axis=0)
                got = (dot(pick, gy_j) * gate).astype(BF)
                de[:, EP * STRIP * j:EP * STRIP * (j + 1), cols] = got.reshape(LOCAL, EP * STRIP, third)
        xe_copy.start()
        de_copy.start()
        x_s = jnp.concatenate([all_ref[g * TP + j, :TOK, :] for j in range(TP)], axis=0)
        gy_s = jnp.concatenate([all_ref[g * TP + j, TOK:, :] for j in range(TP)], axis=0)
        a = dot(x_s, wsg_ref[...]).astype(BF).astype(F32)
        b = dot(x_s, wsu_ref[...]).astype(BF).astype(F32)
        dh = dot_nt(gy_s, wsd_ref[...]).astype(BF).astype(F32)
        h, da, db = act_both(a, b, dh)
        for n in range(3):
            cols = slice(n * third, (n + 1) * third)
            sh[0, :, :, cols] = dot(h, wsd_ref[:, cols]).reshape(TP, TOK, third)
            dxs = dot_nt(da, wsg_ref[cols, :]) + dot_nt(db, wsu_ref[cols, :])
            sh[1, :, :, cols] = dxs.reshape(TP, TOK, third)

    lhs = []
    for i in range(2):
        e = 2 * step + i
        x_e = xe[e]
        ab = dot(x_e, jnp.concatenate([wg_ref[i], wu_ref[i]], axis=1)).astype(BF).astype(F32)
        dh = dot_nt(de[e], wd_ref[i]).astype(BF).astype(F32)
        width = ab.shape[1] // 2
        h, da, db = act_both(ab[:, :width], ab[:, width:], dh)
        h_ref[i] = h
        dab = jnp.concatenate([da, db], axis=1)
        dab_ref[i] = dab
        lhs.append(dot(perm_ref[i], dab).astype(BF))
    lhs = jnp.concatenate(lhs, axis=1)
    for n in range(3):
        cols = slice(n * third, (n + 1) * third)
        rhs = jnp.concatenate([wg_ref[0, cols, :], wu_ref[0, cols, :], wg_ref[1, cols, :], wu_ref[1, cols, :]], axis=1)
        part_ref[:, :PAIR_ROWS, cols] = dot_nt(lhs, rhs).reshape(TP, PAIR_ROWS, third)
    half = step // (STEPS // 2)
    first = pl.multiple_of((step % (STEPS // 2)) * SH_ROWS, SH_ROWS)
    part_ref[:, PAIR_ROWS:, :] = sh[half, :, pl.ds(first, SH_ROWS), :]

    @pl.when(step == STEPS - 1)
    def _():
        xe_copy.wait()
        de_copy.wait()


def main_call(g, all_rows, slots, w_router, ws_gate, ws_up, ws_down, perm, w_gate, w_up, w_down):
    width = w_gate.shape[2]

    def whole(a):
        return pl.BlockSpec(a.shape, lambda i, g_: (0,) * a.ndim, pipeline_mode=pl.Buffered(1))

    def pair(a):
        return pl.BlockSpec((2,) + a.shape[1:], lambda i, g_: (i, 0, 0))

    any_spec = pl.BlockSpec(memory_space=pl.ANY)
    return pl.pallas_call(
        main_kernel,
        name='main_call',
        grid_spec=pltpu.PrefetchScalarGridSpec(
            num_scalar_prefetch=1,
            grid=(STEPS,),
            in_specs=[whole(all_rows), whole(slots), whole(w_router), whole(ws_gate), whole(ws_up), whole(ws_down), whole(perm),
                      pair(w_gate), pair(w_up), pair(w_down)],
            out_specs=[pl.BlockSpec((TP, BLK, D), lambda i, g_: (0, i, 0)),
                       pl.BlockSpec((2, ROWS, width), lambda i, g_: (i, 0, 0)),
                       pl.BlockSpec((2, ROWS, 2 * width), lambda i, g_: (i, 0, 0)), any_spec, any_spec],
            scratch_shapes=[pltpu.VMEM((LOCAL, ROWS, D), BF), pltpu.VMEM((LOCAL, ROWS, D), BF),
                            pltpu.VMEM((2, TP, TOK, D), F32), pltpu.SemaphoreType.DMA((2,))],
        ),
        out_shape=[jax.ShapeDtypeStruct((TP, BLK * STEPS, D), F32), jax.ShapeDtypeStruct((LOCAL, ROWS, width), BF),
                   jax.ShapeDtypeStruct((LOCAL, ROWS, 2 * width), BF),
                   jax.ShapeDtypeStruct((LOCAL, ROWS, D), BF), jax.ShapeDtypeStruct((LOCAL, ROWS, D), BF)],
        compiler_params=pltpu.CompilerParams(vmem_limit_bytes=58 << 20),
        cost_estimate=pl.CostEstimate(flops=20_000_000_000, bytes_accessed=60_000_000, transcendentals=4_000_000),
    )(g, all_rows, slots, w_router, ws_gate, ws_up, ws_down, perm, w_gate, w_up, w_down)


def grad_kernel(xe_ref, de_ref, h_ref, dab_ref, dg_ref, du_ref, dd_ref):
    both = dot_tn(xe_ref[0], dab_ref[0])
    width = both.shape[1] // 2
    dg_ref[0] = both[:, :width]
    du_ref[0] = both[:, width:]
    dd_ref[0] = dot_tn(h_ref[0], de_ref[0])


def grad_call(xe, de, h, dab):
    width = h.shape[2]

    def one(shape):
        return pl.BlockSpec((1,) + shape, lambda i: (i, 0, 0))

    return pl.pallas_call(
        grad_kernel,
        name='grad_call',
        grid=(LOCAL,),
        in_specs=[one((ROWS, D)), one((ROWS, D)), one((ROWS, width)), one((ROWS, 2 * width))],
        out_specs=[one((D, width)), one((D, width)), one((width, D))],
        out_shape=[jax.ShapeDtypeStruct((LOCAL, D, width), F32), jax.ShapeDtypeStruct((LOCAL, D, width), F32),
                   jax.ShapeDtypeStruct((LOCAL, width, D), F32)],
        compiler_params=pltpu.CompilerParams(vmem_limit_bytes=40 << 20),
        cost_estimate=pl.CostEstimate(flops=10_000_000_000, bytes_accessed=55_000_000, transcendentals=0),
    )(xe, de, h, dab)


def out_kernel(tp_ref, h0, h1, h2, h3, w0, w1, w2, w3, o_ref):
    total = dot(jnp.concatenate([h0[0], h1[0], h2[0], h3[0]], axis=1), jnp.concatenate([w0[0], w1[0], w2[0], w3[0]], axis=0))
    for j in range(TP):
        for s in range(EP):
            first = STRIP * (j * EP + s)
            o_ref[s * TP + j, 0] = total[first:first + STRIP].astype(BF)


def out_call(tp, h_own, h_in, w_own, w_in):
    width = h_own.shape[2]
    per = LOCAL // TP

    def own(shape):
        return pl.BlockSpec((1,) + shape, lambda i, t: (t[0] * per + i, 0, 0))

    def got(shape):
        return pl.BlockSpec((1,) + shape, lambda i, t: (i, 0, 0))

    return pl.pallas_call(
        out_kernel,
        name='out_call',
        grid_spec=pltpu.PrefetchScalarGridSpec(
            num_scalar_prefetch=1,
            grid=(per,),
            in_specs=[own((ROWS, width))] + [got((ROWS, width))] * 3 + [own((width, D))] + [got((width, D))] * 3,
            out_specs=pl.BlockSpec((NDEV, 1, STRIP, D), lambda i, t: (0, i, 0, 0)),
        ),
        out_shape=jax.ShapeDtypeStruct((NDEV, per, STRIP, D), BF),
        compiler_params=pltpu.CompilerParams(vmem_limit_bytes=40 << 20),
        cost_estimate=pl.CostEstimate(flops=5_000_000_000, bytes_accessed=10_000_000, transcendentals=0),
    )(tp, h_own, *h_in, w_own, *w_in)


def permutations():
    row = jnp.arange(TP * PAIR_ROWS)
    col, rest = row // PAIR_ROWS, row % PAIR_ROWS
    src, rest = rest // (2 * CAP), rest % (2 * CAP)
    which, slot = rest // CAP, rest % CAP
    wanted = col * (EP * STRIP) + src * STRIP + slot
    hit = wanted[:, None] == jnp.arange(ROWS)[None, :]
    return jnp.stack([hit & (which == i)[:, None] for i in range(2)]).astype(BF)


def solution(mesh):
    def device_step(x, grad_y, w_router, w_gate, w_up, w_down, ws_gate, ws_up, ws_down, topk_idx):
        tp = lax.axis_index('tp')
        ep = lax.axis_index('ep')
        per = LOCAL // TP
        w_down_in = []
        for m in range(1, TP):
            away = lax.dynamic_slice_in_dim(w_down, (tp ^ m) * per, per, axis=0)
            w_down_in.append(lax.ppermute(away, 'tp', [(s, s ^ m) for s in range(TP)]))

        ids = jnp.arange(EXPERTS, dtype=jnp.int32)
        hit = jnp.any(topk_idx[:, :, None] == ids[None, None, :], axis=1)
        before = jnp.tril(jnp.ones((TOK, TOK), BF), -1)
        rank = dot(before, hit.astype(BF))
        rank = jnp.where(hit, rank, -1.0).astype(jnp.int32)
        slot_hit = rank[:, :, None] == jnp.arange(STRIP, dtype=jnp.int32)[None, None, :]
        token = jnp.arange(TOK, dtype=jnp.int32)[:, None, None] + 1
        table = jnp.sum(jnp.where(slot_hit, token, 0), axis=0, dtype=jnp.int32) - 1
        table = jnp.concatenate([table.reshape(EP, LOCAL * STRIP), jnp.zeros((8 - EP, LOCAL * STRIP), jnp.int32)], axis=0)
        all_rows, tables = gather_rows(jnp.concatenate([x, grad_y], axis=0), table)
        mine = lax.dynamic_index_in_dim(tables, ep, 1, keepdims=False).reshape(EP, TP, LOCAL, STRIP)
        base = (TOK * jnp.arange(EP, dtype=jnp.int32))[:, None, None, None]
        slots = jnp.where(mine >= 0, mine + base, -1).transpose(1, 2, 0, 3).reshape(TP, LOCAL * EP * STRIP, 1)

        parts, h, dab, xe, de = main_call(ep.reshape(1), all_rows, slots, w_router, ws_gate, ws_up, ws_down, permutations(), w_gate, w_up, w_down)
        summed = lax.psum_scatter(parts, 'tp', scatter_dimension=0).reshape(STEPS, BLK, D)

        h_in = []
        for m in range(1, TP):
            away = lax.dynamic_slice_in_dim(h, (tp ^ m) * per, per, axis=0)
            h_in.append(lax.ppermute(away, 'tp', [(s, s ^ m) for s in range(TP)]))
        o_send = out_call(tp.reshape(1), h, h_in, w_down, w_down_in)
        o_rows = lax.all_to_all(o_send, ('ep', 'tp'), 0, 0).reshape(EXPERTS * STRIP, D)

        d_w_gate, d_w_up, d_w_down = grad_call(xe, de, h, dab)

        x_all = all_rows[:, :TOK].reshape(NDEV * TOK, D)
        gy_all = all_rows[:, TOK:].reshape(NDEV * TOK, D)
        sa = dot(x_all, ws_gate).astype(BF).astype(F32)
        sb = dot(x_all, ws_up).astype(BF).astype(F32)
        sdh = dot_nt(gy_all, ws_down).astype(BF).astype(F32)
        s_h, s_da, s_db = act_both(sa, sb, sdh)
        ds_gate = dot_tn(x_all, s_da)
        ds_up = dot_tn(x_all, s_db)
        ds_down = dot_tn(s_h, gy_all)

        probs = jax.nn.softmax(dot(x, w_router), axis=-1)
        scaled = GATE_SCALE * probs
        gate_slot = jnp.where(slot_hit, scaled[:, :, None], 0.0).reshape(TOK, EXPERTS * STRIP)
        routed = jnp.dot(gate_slot, o_rows.astype(F32), precision=lax.Precision.HIGHEST)
        seen = dot_nt(grad_y, o_rows).reshape(TOK, EXPERTS, STRIP)
        d_scores = GATE_SCALE * jnp.sum(jnp.where(slot_hit, seen, 0.0), axis=2)
        d_logits = probs * (d_scores - jnp.sum(probs * d_scores, axis=-1, keepdims=True))
        d_logits_all = lax.all_gather(d_logits, ('ep', 'tp'), axis=0, tiled=True)
        d_router = lax.dot_general(x_all.astype(F32), d_logits_all, (((0,), (0,)), ((), ())), precision=lax.Precision.HIGHEST)
        dx_router = lax.dot_general(d_logits, w_router.astype(F32), (((1,), (1,)), ((), ())), precision=lax.Precision.HIGHEST)

        half = STEPS // 2
        shared = summed[:half, PAIR_ROWS:].reshape(TOK, D)
        dx_shared = summed[half:, PAIR_ROWS:].reshape(TOK, D)
        y_out = (shared + routed).astype(BF)
        own = summed[:, :PAIR_ROWS].astype(BF).reshape(STEPS, EP, 2 * CAP, D).transpose(1, 0, 2, 3)
        back = lax.all_to_all(own, 'ep', 0, 0).reshape(EXPERTS * CAP, D)
        mark = slot_hit[:, :, :CAP].reshape(TOK, EXPERTS * CAP).astype(BF)
        dx_out = (dx_router + dx_shared + dot(mark, back)).astype(BF)
        return y_out, dx_out, d_router, d_w_gate, d_w_up, d_w_down, ds_gate, ds_up, ds_down

    tok_spec = P(('ep', 'tp'), None)
    in_specs = (tok_spec, tok_spec, P(None, None), P('ep', None, 'tp'), P('ep', None, 'tp'), P('ep', 'tp', None), P(None, 'tp'), P(None, 'tp'), P('tp', None), tok_spec)
    out_specs = (tok_spec, tok_spec, P(None, None), P('ep', None, 'tp'), P('ep', None, 'tp'), P('ep', 'tp', None), P(None, 'tp'), P(None, 'tp'), P('tp', None))
    return jax.shard_map(device_step, mesh=mesh, in_specs=in_specs, out_specs=out_specs, check_vma=False)
```

time: 663 us -> 333 us (0.50)
  waiting for transfers between devices: 326 us -> 143 us
  matrix products: 113 us -> 22.5 us
  Pallas kernels: 0 us -> 77.4 us
  local copies, waits for them, and re-layouts: 96.3 us -> 27.8 us
  blocking collectives: 75.5 us -> 27.8 us
  other arithmetic: 21.5 us -> 4.86 us
    unnamed x10 -> x2, waiting for transfers between devices: 160 us -> 3.24 us
    ppermute x0 -> x6, waiting for transfers between devices: none -> 128 us  [the longest x3 128 us: device_step(): h_in.append(lax.ppermute(away, 'tp', [(s, s ^ m) for s in range(TP)]))]
    dot_general x23 -> x13, matrix products: 113 us -> 22.5 us  [the longest x3 9.21 us: dot_tn(): lax.dot_general(a, b, (((0,), (0,)), ((), ())), preferred_element_type=F32)]
    all_gather x2 -> x0, waiting for transfers between devices: 85 us -> none  [the longest x1 59.9 us: device_step(): expert_rows = lax.all_gather(recv_rows, 'tp', axis=0)]
    pallas_call x0 -> x4, Pallas kernels: none -> 77.4 us  [the longest x1 29.4 us: main_call(): pl.pallas_call(main_kernel, name='main_call', grid_spec=pltpu.PrefetchSca...]
    psum x2 -> x0, waiting for transfers between devices: 66.9 us -> none  [the longest x1 62.9 us: device_step(): lax.psum(jnp.einsum('td,te->de', x, d_logits, preferred_element_type=jnp....]
    all_to_all x2 -> x0, blocking collectives: 43.2 us -> none  [the longest x1 22.2 us: device_step(): recv_rows = lax.all_to_all(send_rows, 'ep', 0, 0)]
    gather x14 -> x0, local copies, waits for them, and re-layouts: 21.6 us -> none  [the longest x2 5.01 us: device_step(): picked = jnp.take(back_rows, slot_of, axis=0)]
  transfers between devices with their start and end apart: 10 -> 9, of which waited for: 7 -> 5; matrix products, arithmetic and copies ran while one was open for 22% -> 9% of each run, Pallas kernels for 0% -> 6%
where the time goes in v1:
time: 333 us; the launch traced here: 332 us
  waiting for transfers between devices  143 us (43%)
  Pallas kernels  77.4 us (23%)
  local copies, waits for them, and re-layouts  27.8 us (8%)
  blocking collectives  27.8 us (8%)
  matrix products  22.5 us (7%)
  starting transfers between devices  14.4 us (4%)
  between operations  14.4 us (4%)
  other arithmetic  4.86 us (1%)
    ppermute x3, waiting for transfers between devices, device_step(): h_in.append(lax.ppermute(away, 'tp', [(s, s ^ m) for s in range(TP)]))  128 us
    pallas_call x1, Pallas kernels, main_call(): pl.pallas_call(main_kernel, name='main_call', grid_spec=pltpu.PrefetchSca...  29.4 us
    pallas_call x1, Pallas kernels, gather_rows(): pl.pallas_call(gather_kernel, name='gather_rows', out_shape=(jax.ShapeDty...  27.8 us
    all_gather x1, blocking collectives, device_step(): d_logits_all = lax.all_gather(d_logits, ('ep', 'tp'), axis=0, tiled=True)  27.8 us
    pallas_call x1, Pallas kernels, grad_call(): pl.pallas_call(grad_kernel, name='grad_call', grid=(LOCAL,), in_specs=[on...  15.6 us
    unnamed x41, local copies, waits for them, and re-layouts  14 us
    dot_general x3, matrix products, dot_tn(): lax.dot_general(a, b, (((0,), (0,)), ((), ())), preferred_element_type=F32)  9.21 us
    all_to_all x1, waiting for transfers between devices, device_step(): back = lax.all_to_all(own, 'ep', 0, 0).reshape(EXPERTS * CAP, D)  8.98 us
  transfers between devices with their start and end apart: 9, of which 5 were waited for; matrix products, arithmetic and copies ran while one was open for 9% of the time, Pallas kernels for 6%

profile of v1, /device:TPU:0, one launch (start us, length us, event | category | flops | bytes accessed | tf_op | source)
XLA Modules:
  0.0 332.5 jit_solution(6933499792146665905)
XLA Ops:
  9.7 1.9 copy.52.wr_ref
  12.6 27.8 %gather_rows.1 = (bf16[16,128,1536]{2,1,0:T(8,128)(2,1)S(1)}, s32[16,8,128]{2,1,0:T(8,128)S(1)}) custom-call(bf16[128,1536]{1,0:T(8,128)(2,1)S(1)} %pad_maximum_fusion.rows_ref, s32[8,128]{1,0:T(8,128)S(1)} %concatenate.7.tab_ref), custom_call_target="tpu_custom_call" | custom-call | flops 40000000000 | bytes 7000000 | tf_op jit(solution)/shard_map/gather_rows/pallas_call | solution.py:153
  40.4 2.7 copy-done
  45.6 29.4 %main_call.1 = (f32[4,576,1536]{2,1,0:T(8,128)}, bf16[16,128,128]{2,1,0:T(8,128)(2,1)}, bf16[16,128,256]{2,1,0:T(8,128)(2,1)}, bf16[16,128,1536]{2,1,0:T(8,128)(2,1)}, bf16[16,128,1536]{2,1,0:T(8,128)(2,1)}) custom-call(s32[1]{0:T(128)} %bitcast.g_ref, bf16[16,128,1536]{2,1,0:T(8,128)(2,1)} %copy-done, s32[4,512,1]{2,1,0:T(8,128)} %reshape.274.slot_ref, ...), custom_call_target="tpu_custom_call" | custom-call | flops 20000000000 | bytes 60000000 | tf_op jit(solution)/shard_map/main_call/pallas_call | solution.py:251
  75.0 5.0 %constant_dynamic-slice_fusion = (bf16[4,128,1536]{2,1,0:T(8,128)(2,1)}, bf16[4,128,1536]{2,1,0:T(8,128)(2,1)}, bf16[4,128,1536]{2,1,0:T(8,128)(2,1)}) fusion(bf16[16,128,1536]{2,1,0:T(8,128)(2,1)} %w0.1, s32[]{:T(128)S(6)} %select_n.142, s32[]{:T(128)S(6)} %select_n.141, s32[]{:T(128)S(6)} %select_n.140), kind=kLoop, calls=%fused_computation.70 | loop fusion | bytes 9437196 | tf_op jit(solution)/shard_map/dynamic_slice | solution.py:350
  91.3 2.2 fusion.14
  93.5 2.3 fusion.16
  96.0 121.9 %collective-permute-done.2.h3 = bf16[4,128,128]{2,1,0:T(8,128)(2,1)S(1)} collective-permute-done((bf16[4,128,128]{2,1,0:T(8,128)(2,1)S(1)}, bf16[4,128,128]{2,1,0:T(8,128)(2,1)S(1)}, u32[]{:S(2)}, u32[]{:S(2)}) %collective-permute-start.2) | collective-permute-done | bytes 131104 | tf_op jit(solution)/shard_map/ppermute | solution.py:373
  220.4 6.2 %collective-permute-done.h1 = bf16[4,128,128]{2,1,0:T(8,128)(2,1)S(1)} collective-permute-done((bf16[4,128,128]{2,1,0:T(8,128)(2,1)S(1)}, bf16[4,128,128]{2,1,0:T(8,128)(2,1)S(1)}, u32[]{:S(2)}, u32[]{:S(2)}) %collective-permute-start) | collective-permute-done | bytes 131104 | tf_op jit(solution)/shard_map/ppermute | solution.py:373
  226.7 2.8 copy-done.2
  229.4 4.7 %out_call.1 = bf16[16,4,8,1536]{3,2,1,0:T(8,128)(2,1)} custom-call(s32[1]{0:T(128)} %bitcast.5.tp_ref, bf16[16,128,128]{2,1,0:T(8,128)(2,1)S(1)} %copy-done.3, bf16[4,128,128]{2,1,0:T(8,128)(2,1)S(1)} %collective-permute-done.h1, bf16[4,128,128]{2,1,0:T(8,128)(2,1)S(1)} %collective-permute-done.1.h2, bf16[4,128,128]{2,1,0:T(8,128)(2,1)S(1)} %collective-permute-done.2.h3, ...), custom_call_target="tpu_custom_call" | custom-call | flops 5000000000 | bytes 10000000 | tf_op jit(solution)/shard_map/out_call/pallas_call | solution.py:318
  234.1 2.4 all-to-all-start
  236.6 4.7 %fusion.12 = f32[1536,256]{1,0:T(8,128)} fusion(bf16[1024,1536]{1,0:T(8,128)(2,1)} %bitcast.52, bf16[1024,256]{1,0:T(8,128)(2,1)} %copy-done.18, bf16[1024,256]{1,0:T(8,128)(2,1)} %copy-done.19, bf16[1024,256]{1,0:T(8,128)(2,1)} %copy-done.17), kind=kOutput, calls=%fused_computation.27 | convolution fusion | flops 808714240 | bytes 6291456 | tf_op jit(solution)/shard_map/dot_general | solution.py:54
  241.3 2.8 copy-done.4
  244.1 2.8 copy-done.5
  246.9 15.6 %grad_call.1 = (f32[16,1536,128]{2,1,0:T(8,128)}, f32[16,1536,128]{2,1,0:T(8,128)}, f32[16,128,1536]{2,1,0:T(8,128)}) custom-call(bf16[16,128,1536]{2,1,0:T(8,128)(2,1)S(1)} %copy-done.4, bf16[16,128,1536]{2,1,0:T(8,128)(2,1)S(1)} %copy-done.5, bf16[16,128,128]{2,1,0:T(8,128)(2,1)S(1)} %copy-done.3, bf16[16,128,256]{2,1,0:T(8,128)(2,1)S(1)} %copy-done.6), custom_call_target="tpu_custom_call" | custom-call | flops 10000000000 | bytes 55000000 | tf_op jit(solution)/shard_map/grad_call/pallas_call | solution.py:287
  262.5 2.9 all-to-all-done
  267.0 27.8 %all_gather.3 = f32[1024,64]{1,0:T(8,128)S(1)} all-gather(f32[64,64]{1,0:T(8,128)S(1)} %copy.56), channel_id=1, replica_groups=mesh['tp'=4,'ep'=4] {'ep','tp'}, dimensions={0}, use_global_device_ids=true | all-gather | bytes 278528 | tf_op jit(solution)/shard_map/all_gather | solution.py:396
  294.8 3.2 reduce-scatter.4.cloned.1.call-done
  298.0 1.9 slice.30
  301.4 3.8 %all-to-all-start.1 = ((bf16[4,8,14,1536]{3,1,2,0:T(8,128)(2,1)}), bf16[4,8,14,1536]{3,1,2,0:T(8,128)(2,1)S(1)}, u32[]{:S(2)}, u32[]{:S(2)}) async-start(bf16[4,8,14,1536]{3,1,2,0:T(8,128)(2,1)} %bitcast.54), calls=%async_computation.1 | async-start | bytes 2752512 | tf_op jit(solution)/shard_map/all_to_all | solution.py:405
  305.2 4.5 %fusion.49 = f32[1536,64]{0,1:T(8,128)} fusion(bf16[1024,1536]{1,0:T(8,128)(2,1)} %bitcast.53, f32[1024,64]{1,0:T(8,128)S(1)} %all_gather.3), kind=kOutput, calls=%fused_computation.97 | convolution fusion | flops 1207959552 | bytes 3801088 | tf_op jit(solution)/shard_map/dot_general | solution.py:397
  313.7 9.0 %all-to-all-done.1 = bf16[4,8,14,1536]{3,1,2,0:T(8,128)(2,1)S(1)} async-done(((bf16[4,8,14,1536]{3,1,2,0:T(8,128)(2,1)}), bf16[4,8,14,1536]{3,1,2,0:T(8,128)(2,1)S(1)}, u32[]{:S(2)}, u32[]{:S(2)}) %all-to-all-start.1) | async-done | bytes 1376288 | tf_op jit(solution)/shard_map/all_to_all | solution.py:405
  323.6 2.1 fusion.1
  (89 shorter events, 27.8 us)
Async XLA Ops:
  7.2 290.8 %reduce-scatter.4.cloned.1.call-start = ((), (), s32[]{:S(2)}) async-start(), calls=%async_computation.3 | async-start | bytes 17694720
  40.4 2.7 copy-start
  75.0 8.5 %copy-start.3 = (bf16[16,128,128]{2,1,0:T(8,128)(2,1)S(1)}, bf16[16,128,128]{2,1,0:T(8,128)(2,1)}, u32[]{:S(2)}) copy-start(bf16[16,128,128]{2,1,0:T(8,128)(2,1)} %get-tuple-element.22.h0.h_ref) | copy-start | bytes 1572868
  75.0 11.5 %copy-start.1 = (bf16[16,128,1536]{2,1,0:T(8,128)(2,1)S(1)}, bf16[16,128,1536]{2,1,0:T(8,128)(2,1)}, u32[]{:S(2)}) copy-start(bf16[16,128,1536]{2,1,0:T(8,128)(2,1)} %copy-done) | copy-start | bytes 18874372
  80.1 146.6 %collective-permute-start.5 = (bf16[4,128,1536]{2,1,0:T(8,128)(2,1)}, bf16[4,128,1536]{2,1,0:T(8,128)(2,1)S(1)}, u32[]{:S(2)}, u32[]{:S(2)}) collective-permute-start(bf16[4,128,1536]{2,1,0:T(8,128)(2,1)} %get-tuple-element.31), channel_id=1, source_target_pairs={{0,12},{4,8},{8,4},{12,0},{1,13},{5,9},{9,5},{13,1},{2,14},{6,10},... | collective-permute-start | bytes 4718600 | tf_op jit(solution)/shard_map/ppermute | solution.py:351
  81.5 145.1 %collective-permute-start.4 = (bf16[4,128,1536]{2,1,0:T(8,128)(2,1)}, bf16[4,128,1536]{2,1,0:T(8,128)(2,1)}, u32[]{:S(2)}, u32[]{:S(2)}) collective-permute-start(bf16[4,128,1536]{2,1,0:T(8,128)(2,1)} %get-tuple-element.32), channel_id=1, source_target_pairs={{0,8},{4,12},{8,0},{12,4},{1,9},{5,13},{9,1},{13,5},{2,10},{6,14},... | collective-permute-start | bytes 4718600 | tf_op jit(solution)/shard_map/ppermute | solution.py:351
  83.0 143.6 %collective-permute-start.3 = (bf16[4,128,1536]{2,1,0:T(8,128)(2,1)}, bf16[4,128,1536]{2,1,0:T(8,128)(2,1)}, u32[]{:S(2)}, u32[]{:S(2)}) collective-permute-start(bf16[4,128,1536]{2,1,0:T(8,128)(2,1)} %get-tuple-element.33), channel_id=1, source_target_pairs={{0,4},{4,0},{8,12},{12,8},{1,5},{5,1},{9,13},{13,9},{2,6},{6,2},{1... | collective-permute-start | bytes 4718600 | tf_op jit(solution)/shard_map/ppermute | solution.py:351
  83.6 134.3 %collective-permute-start.2 = (bf16[4,128,128]{2,1,0:T(8,128)(2,1)S(1)}, bf16[4,128,128]{2,1,0:T(8,128)(2,1)S(1)}, u32[]{:S(2)}, u32[]{:S(2)}) collective-permute-start(bf16[4,128,128]{2,1,0:T(8,128)(2,1)S(1)} %get-tuple-element.36), channel_id=1, source_target_pairs={{0,12},{4,8},{8,4},{12,0},{1,13},{5,9},{9,5},{13,1},{2,14},{6,10},... | collective-permute-start | bytes 393224 | tf_op jit(solution)/shard_map/ppermute | solution.py:373
  85.1 135.3 %collective-permute-start.1 = (bf16[4,128,128]{2,1,0:T(8,128)(2,1)S(1)}, bf16[4,128,128]{2,1,0:T(8,128)(2,1)S(1)}, u32[]{:S(2)}, u32[]{:S(2)}) collective-permute-start(bf16[4,128,128]{2,1,0:T(8,128)(2,1)S(1)} %get-tuple-element.37), channel_id=1, source_target_pairs={{0,8},{4,12},{8,0},{12,4},{1,9},{5,13},{9,1},{13,5},{2,10},{6,14},... | collective-permute-start | bytes 393224 | tf_op jit(solution)/shard_map/ppermute | solution.py:373
  87.2 6.3 %copy-start.7 = (bf16[16,64,1536]{2,1,0:T(8,128)(2,1)}, bf16[16,64,1536]{2,1,0:T(8,128)(2,1)S(1)}, u32[]{:S(2)}) copy-start(bf16[16,64,1536]{2,1,0:T(8,128)(2,1)S(1)} %get-tuple-element.30) | copy-start | bytes 9437188
  89.0 4.5 %copy-start.17 = (bf16[1024,256]{1,0:T(8,128)(2,1)}, bf16[1024,256]{1,0:T(8,128)(2,1)S(1)}, u32[]{:S(2)}) copy-start(bf16[1024,256]{1,0:T(8,128)(2,1)S(1)} %convolution_convert_fusion) | copy-start | bytes 1572868
  93.5 2.3 copy-start.8
  93.5 2.3 copy-start.11
  217.9 8.7 %collective-permute-start = (bf16[4,128,128]{2,1,0:T(8,128)(2,1)S(1)}, bf16[4,128,128]{2,1,0:T(8,128)(2,1)S(1)}, u32[]{:S(2)}, u32[]{:S(2)}) collective-permute-start(bf16[4,128,128]{2,1,0:T(8,128)(2,1)S(1)} %get-tuple-element.38), channel_id=1, source_target_pairs={{0,4},{4,0},{8,12},{12,8},{1,5},{5,1},{9,13},{13,9},{2,6},{6,2},{1... | collective-permute-start | bytes 393224 | tf_op jit(solution)/shard_map/ppermute | solution.py:373
  226.7 2.8 copy-start.2
  234.1 31.3 %all-to-all-start = ((bf16[16,4,8,1536]{3,2,1,0:T(8,128)(2,1)}), bf16[16,4,8,1536]{3,2,1,0:T(8,128)(2,1)S(1)}, u32[]{:S(2)}, u32[]{:S(2)}) async-start(bf16[16,4,8,1536]{3,2,1,0:T(8,128)(2,1)} %out_call.1), calls=%async_computation | async-start | bytes 3145728 | tf_op jit(solution)/shard_map/all_to_all | solution.py:375
  236.6 4.7 %copy-start.6 = (bf16[16,128,256]{2,1,0:T(8,128)(2,1)S(1)}, bf16[16,128,256]{2,1,0:T(8,128)(2,1)}, u32[]{:S(2)}) copy-start(bf16[16,128,256]{2,1,0:T(8,128)(2,1)} %get-tuple-element.25.dab_ref) | copy-start | bytes 3145732
  241.3 2.8 copy-start.4
  244.1 2.8 copy-start.5
  246.9 18.5 %copy-start.10 = (bf16[64,1536]{1,0:T(8,128)(2,1)S(1)}, bf16[64,1536]{1,0:T(8,128)(2,1)}, u32[]{:S(2)}) copy-start(bf16[64,1536]{1,0:T(8,128)(2,1)} %param.11) | copy-start | bytes 589828
  301.4 21.3 %all-to-all-start.1 = ((bf16[4,8,14,1536]{3,1,2,0:T(8,128)(2,1)}), bf16[4,8,14,1536]{3,1,2,0:T(8,128)(2,1)S(1)}, u32[]{:S(2)}, u32[]{:S(2)}) async-start(bf16[4,8,14,1536]{3,1,2,0:T(8,128)(2,1)} %bitcast.54), calls=%async_computation.1 | async-start | bytes 2752512 | tf_op jit(solution)/shard_map/all_to_all | solution.py:405
  305.2 5.7 %copy-start.9 = (bf16[1536,64]{0,1:T(8,128)(2,1)S(1)}, bf16[1536,64]{0,1:T(8,128)(2,1)}, u32[]{:S(2)}) copy-start(bf16[1536,64]{0,1:T(8,128)(2,1)} %param.12) | copy-start | bytes 589828
  305.2 6.8 %copy-start.13 = (f32[64,64]{0,1:T(8,128)S(1)}, f32[64,64]{0,1:T(8,128)}, u32[]{:S(2)}) copy-start(f32[64,64]{0,1:T(8,128)} %get-tuple-element.40) | copy-start | bytes 49156
  313.7 9.9 %copy-start.12 = (pred[64,448]{0,1:T(32,128)(4,1)S(1)}, pred[64,448]{0,1:T(32,128)(4,1)}, u32[]{:S(2)}) copy-start(pred[64,448]{0,1:T(32,128)(4,1)} %reshape.269) | copy-start | bytes 86020
  (5 other events, 8.7 us)
Sparse Core Ops, SparseCore 0:
  75.1 222.8 reduce-scatter.3

commit v2 on v1

--- a/solution.py
+++ b/solution.py
@@ -1,5 +1,3 @@
-import functools
-
 import jax
 import jax.numpy as jnp
 from jax import lax
@@ -7,6 +5,7 @@
 from jax.experimental.pallas import tpu as pltpu
 from jax.sharding import PartitionSpec as P
 
+
 GATE_SCALE = 16.0
 BF = jnp.bfloat16
 F32 = jnp.float32
@@ -14,7 +13,6 @@
 
 D = 1536
 EXPERTS = 64
-TOP = 6
 TOK = 64
 TP = 4
 EP = 4
@@ -27,6 +25,9 @@
 STEPS = LOCAL // 2
 SH_ROWS = 2 * TOK // STEPS
 BLK = PAIR_ROWS + SH_ROWS
+CHUNKS = 2
+PER_CHUNK = STEPS // CHUNKS
+EARLY = 2
 
 BIT_Y, BIT_Z, BIT_C, BIT_X = 1, 2, 4, 8
 
@@ -63,7 +64,7 @@
     return h, da, db
 
 
-def gather_kernel(rows_ref, tab_ref, all_ref, tabs_ref, send_sem, recv_sem, local_sem):
+def gather_kernel(rows_ref, tab_ref, w_ref, all_ref, tabs_ref, w_in_ref, keep_ref, send_sem, recv_sem, local_sem, w_send, w_recv, keep_sem):
     tp = lax.axis_index('tp')
     ep = lax.axis_index('ep')
     me = ep * TP + tp
@@ -73,9 +74,17 @@
         return (flip_mask(tp, mask & 3), flip_mask(ep, mask >> 2))
 
     barrier = pltpu.get_barrier_semaphore()
-    for mask in (BIT_X, BIT_Y, BIT_Z, BIT_C):
+    for mask in (BIT_X, BIT_Y, BIT_Z, BIT_C, BIT_Y | BIT_Z):
         pl.semaphore_signal(barrier, inc=1, device_id=peer(mask), device_id_type=MESH)
-    pl.semaphore_wait(barrier, 4)
+    pl.semaphore_wait(barrier, 5)
+
+    sent = []
+    for m in range(1, TP):
+        first = flip_mask(tp, m) * (LOCAL // TP)
+        c = pltpu.make_async_remote_copy(src_ref=w_ref.at[pl.ds(first, EARLY)], dst_ref=w_in_ref.at[m - 1],
+                                         send_sem=w_send.at[m - 1], recv_sem=w_recv.at[m - 1], device_id=peer(m), device_id_type=MESH)
+        c.start()
+        sent.append(c)
 
     orders = [(BIT_X, BIT_Y, BIT_Z), (BIT_Y, BIT_Z, BIT_X), (BIT_Z, BIT_X, BIT_Y), (BIT_X, BIT_Y, BIT_Z)]
 
@@ -91,8 +100,6 @@
             src_ref=view(part, block, k == 0), dst_ref=view(part, block, False),
             send_sem=send_sem.at[part, k ^ mask], recv_sem=recv_sem.at[part, k ^ mask],
             device_id=peer(mask), device_id_type=MESH)
-
-    sent = []
 
     def send(part, k, mask):
         c = copy(part, k, mask)
@@ -138,34 +145,51 @@
             k = (m3, m1 ^ m3, m2 ^ m3, m1 ^ m2 ^ m3)[extra]
             arrived(part, k)
             send(part, k, BIT_C)
-    for part in parts:
-        for k in range(16):
-            if k & BIT_C:
-                arrived(part, k)
     own_rows.wait()
     own_tab.wait()
+    kept = []
+    for k in sorted(range(16), key=lambda k: k & BIT_C):
+        if k & BIT_C:
+            for part in parts:
+                arrived(part, k)
+        block = flip_mask(me, k)
+        c = pltpu.make_async_copy(all_ref.at[block], keep_ref.at[block], keep_sem.at[k])
+        c.start()
+        kept.append(c)
+    for c in kept:
+        c.wait()
+    for c in sent[:TP - 1]:
+        c.wait_recv()
     for c in sent:
         c.wait_send()
 
 
-def gather_rows(rows, tab):
+def gather_rows(rows, tab, w_down):
     vmem = pl.BlockSpec(memory_space=pltpu.VMEM)
+    hbm = pl.BlockSpec(memory_space=pltpu.HBM)
     return pl.pallas_call(
         gather_kernel,
         name='gather_rows',
-        out_shape=(jax.ShapeDtypeStruct((NDEV,) + rows.shape, rows.dtype), jax.ShapeDtypeStruct((NDEV,) + tab.shape, tab.dtype)),
-        in_specs=[vmem, vmem],
-        out_specs=(vmem, vmem),
-        scratch_shapes=[pltpu.SemaphoreType.DMA((4, 16)), pltpu.SemaphoreType.DMA((4, 16)), pltpu.SemaphoreType.DMA((2,))],
+        out_shape=(jax.ShapeDtypeStruct((NDEV,) + rows.shape, rows.dtype), jax.ShapeDtypeStruct((NDEV,) + tab.shape, tab.dtype),
+                   jax.ShapeDtypeStruct((TP - 1, EARLY) + w_down.shape[1:], w_down.dtype), jax.ShapeDtypeStruct((NDEV,) + rows.shape, rows.dtype)),
+        in_specs=[vmem, vmem, hbm],
+        out_specs=(vmem, vmem, hbm, hbm),
+        scratch_shapes=[pltpu.SemaphoreType.DMA((4, 16)), pltpu.SemaphoreType.DMA((4, 16)), pltpu.SemaphoreType.DMA((2,)),
+                        pltpu.SemaphoreType.DMA((TP - 1,)), pltpu.SemaphoreType.DMA((TP - 1,)), pltpu.SemaphoreType.DMA((NDEV,))],
         compiler_params=pltpu.CompilerParams(collective_id=0, has_side_effects=True, vmem_limit_bytes=40 << 20),
         cost_estimate=pl.CostEstimate(flops=40_000_000_000, bytes_accessed=7_000_000, transcendentals=0),
-    )(rows, tab)
-
-
-def main_kernel(g_ref, all_ref, slot_ref, wr_ref, wsg_ref, wsu_ref, wsd_ref, perm_ref, wg_ref, wu_ref, wd_ref,
-                part_ref, h_ref, dab_ref, xe_hbm, de_hbm, xe, de, sh, sems):
+    )(rows, tab, w_down)
+
+
+def chunk_members(chunk):
+    return ((0, 1), (2, 3)) if chunk % 2 == 0 else ((0, 2), (1, 3))
+
+
+def main_kernel(g_ref, all_ref, slot_ref, wr_ref, wsg_ref, wsu_ref, wsd_ref, perm_ref, wg_ref, wu_ref, wd_ref, *refs):
+    chunk_refs, (h_ref, dab_ref, xe_hbm, de_hbm, xe, de, sh, sems) = refs[:2 * CHUNKS], refs[2 * CHUNKS:]
     step = pl.program_id(0)
     g = g_ref[0]
+    tp = g_ref[1]
     third = D // 3
     xe_copy = pltpu.make_async_copy(xe, xe_hbm, sems.at[0])
     de_copy = pltpu.make_async_copy(de, de_hbm, sems.at[1])
@@ -224,13 +248,22 @@
         dab_ref[i] = dab
         lhs.append(dot(perm_ref[i], dab).astype(BF))
     lhs = jnp.concatenate(lhs, axis=1)
+    half = step // (STEPS // 2)
+    first = pl.multiple_of((step % (STEPS // 2)) * SH_ROWS, SH_ROWS)
+    found = []
     for n in range(3):
         cols = slice(n * third, (n + 1) * third)
         rhs = jnp.concatenate([wg_ref[0, cols, :], wu_ref[0, cols, :], wg_ref[1, cols, :], wu_ref[1, cols, :]], axis=1)
-        part_ref[:, :PAIR_ROWS, cols] = dot_nt(lhs, rhs).reshape(TP, PAIR_ROWS, third)
-    half = step // (STEPS // 2)
-    first = pl.multiple_of((step % (STEPS // 2)) * SH_ROWS, SH_ROWS)
-    part_ref[:, PAIR_ROWS:, :] = sh[half, :, pl.ds(first, SH_ROWS), :]
+        found.append(dot_nt(lhs, rhs).reshape(TP, PAIR_ROWS, third))
+    for chunk in range(CHUNKS):
+        @pl.when(step // (STEPS // CHUNKS) == chunk)
+        def _(chunk=chunk):
+            for ref, members in zip(chunk_refs[2 * chunk:2 * chunk + 2], chunk_members(chunk)):
+                for at, rel in enumerate(members):
+                    for n in range(3):
+                        ref[at, :PAIR_ROWS, n * third:(n + 1) * third] = found[n][rel]
+                    away = rel ^ tp
+                    ref[at, PAIR_ROWS:, :] = sh[half, away, pl.ds(first, SH_ROWS), :]
 
     @pl.when(step == STEPS - 1)
     def _():
@@ -248,24 +281,27 @@
         return pl.BlockSpec((2,) + a.shape[1:], lambda i, g_: (i, 0, 0))
 
     any_spec = pl.BlockSpec(memory_space=pl.ANY)
+    chunk_specs = [pl.BlockSpec((2, BLK, D), lambda i, g_, c=n // 2: (0, jnp.clip(i - PER_CHUNK * c, 0, PER_CHUNK - 1), 0))
+                   for n in range(2 * CHUNKS)]
     return pl.pallas_call(
         main_kernel,
         name='main_call',
         grid_spec=pltpu.PrefetchScalarGridSpec(
             num_scalar_prefetch=1,
             grid=(STEPS,),
-            in_specs=[whole(all_rows), whole(slots), whole(w_router), whole(ws_gate), whole(ws_up), whole(ws_down), whole(perm),
+            in_specs=[pl.BlockSpec(memory_space=pltpu.VMEM), whole(slots), whole(w_router), whole(ws_gate), whole(ws_up), whole(ws_down), whole(perm),
                       pair(w_gate), pair(w_up), pair(w_down)],
-            out_specs=[pl.BlockSpec((TP, BLK, D), lambda i, g_: (0, i, 0)),
+            out_specs=chunk_specs + [
                        pl.BlockSpec((2, ROWS, width), lambda i, g_: (i, 0, 0)),
                        pl.BlockSpec((2, ROWS, 2 * width), lambda i, g_: (i, 0, 0)), any_spec, any_spec],
             scratch_shapes=[pltpu.VMEM((LOCAL, ROWS, D), BF), pltpu.VMEM((LOCAL, ROWS, D), BF),
                             pltpu.VMEM((2, TP, TOK, D), F32), pltpu.SemaphoreType.DMA((2,))],
         ),
-        out_shape=[jax.ShapeDtypeStruct((TP, BLK * STEPS, D), F32), jax.ShapeDtypeStruct((LOCAL, ROWS, width), BF),
+        out_shape=[jax.ShapeDtypeStruct((2, BLK * PER_CHUNK, D), F32)] * (2 * CHUNKS) + [
+                   jax.ShapeDtypeStruct((LOCAL, ROWS, width), BF),
                    jax.ShapeDtypeStruct((LOCAL, ROWS, 2 * width), BF),
                    jax.ShapeDtypeStruct((LOCAL, ROWS, D), BF), jax.ShapeDtypeStruct((LOCAL, ROWS, D), BF)],
-        compiler_params=pltpu.CompilerParams(vmem_limit_bytes=58 << 20),
+        compiler_params=pltpu.CompilerParams(vmem_limit_bytes=48 << 20),
         cost_estimate=pl.CostEstimate(flops=20_000_000_000, bytes_accessed=60_000_000, transcendentals=4_000_000),
     )(g, all_rows, slots, w_router, ws_gate, ws_up, ws_down, perm, w_gate, w_up, w_down)
 
@@ -297,42 +333,198 @@
     )(xe, de, h, dab)
 
 
-def out_kernel(tp_ref, h0, h1, h2, h3, w0, w1, w2, w3, o_ref):
-    total = dot(jnp.concatenate([h0[0], h1[0], h2[0], h3[0]], axis=1), jnp.concatenate([w0[0], w1[0], w2[0], w3[0]], axis=0))
-    for j in range(TP):
-        for s in range(EP):
-            first = STRIP * (j * EP + s)
-            o_ref[s * TP + j, 0] = total[first:first + STRIP].astype(BF)
-
-
-def out_call(tp, h_own, h_in, w_own, w_in):
+def out_kernel(tp_ref, h0, h1, h2, h3, w_own, e1, e2, e3, l1, l2, l3, o_ref):
+    def emit(e, w1, w2, w3):
+        total = dot(jnp.concatenate([h0[0], h1[0], h2[0], h3[0]], axis=1), jnp.concatenate([w_own[0], w1, w2, w3], axis=0))
+        for j in range(TP):
+            for s in range(EP):
+                first = STRIP * (j * EP + s)
+                o_ref[s * TP + j, STRIP * e:STRIP * (e + 1), :] = total[first:first + STRIP].astype(BF)
+
+    for e in range(LOCAL // TP):
+        @pl.when(pl.program_id(0) == e)
+        def _(e=e):
+            if e < EARLY:
+                emit(e, e1[0, 0], e2[0, 0], e3[0, 0])
+            else:
+                emit(e, l1[0], l2[0], l3[0])
+
+
+def out_call(tp, h_own, h_in, w_down, w_early, w_late):
     width = h_own.shape[2]
     per = LOCAL // TP
-
-    def own(shape):
-        return pl.BlockSpec((1,) + shape, lambda i, t: (t[0] * per + i, 0, 0))
-
-    def got(shape):
-        return pl.BlockSpec((1,) + shape, lambda i, t: (i, 0, 0))
-
     return pl.pallas_call(
         out_kernel,
         name='out_call',
         grid_spec=pltpu.PrefetchScalarGridSpec(
             num_scalar_prefetch=1,
             grid=(per,),
-            in_specs=[own((ROWS, width))] + [got((ROWS, width))] * 3 + [own((width, D))] + [got((width, D))] * 3,
-            out_specs=pl.BlockSpec((NDEV, 1, STRIP, D), lambda i, t: (0, i, 0, 0)),
+            in_specs=[pl.BlockSpec((1, ROWS, width), lambda i, t: (t[0] * per + i, 0, 0))] + [pl.BlockSpec((1, ROWS, width), lambda i, t: (i, 0, 0))] * 3
+            + [pl.BlockSpec((1, width, D), lambda i, t: (t[0] * per + i, 0, 0))]
+            + [pl.BlockSpec((1, 1, width, D), lambda i, t, m=m: (m, jnp.minimum(i, EARLY - 1), 0, 0)) for m in range(TP - 1)]
+            + [pl.BlockSpec((1, width, D), lambda i, t: (jnp.maximum(i - EARLY, 0), 0, 0))] * 3,
+            out_specs=pl.BlockSpec((NDEV, per * STRIP, D), lambda i, t: (0, 0, 0)),
         ),
-        out_shape=jax.ShapeDtypeStruct((NDEV, per, STRIP, D), BF),
+        out_shape=jax.ShapeDtypeStruct((NDEV, per * STRIP, D), BF),
         compiler_params=pltpu.CompilerParams(vmem_limit_bytes=40 << 20),
         cost_estimate=pl.CostEstimate(flops=5_000_000_000, bytes_accessed=10_000_000, transcendentals=0),
-    )(tp, h_own, *h_in, w_own, *w_in)
-
-
-def permutations():
+    )(tp, h_own, *h_in, w_down, w_early, w_early, w_early, *w_late)
+
+
+def split3(v):
+    hi = v.astype(BF)
+    rest = v - hi.astype(F32)
+    mid = rest.astype(BF)
+    return hi, mid, (rest - mid.astype(F32)).astype(BF)
+
+
+def finish_kernel(keep0, keep1, first0, first1, o_ref, x_ref, gy_ref, wr_ref, mark_ref, mark16_ref, all_hbm,
+                  y_ref, dx_ref, drt_ref,
+                  k1, f1, k0, f0, snd, rcv, ret, ret_in, o_in, dl, xa, s_rows, d_rows,
+                  load_sem, x_sem, s2_send, s2_recv, ret_send, ret_recv, o_send, o_recv, dl_send, dl_recv, local_sem):
+    tp = lax.axis_index('tp')
+    ep = lax.axis_index('ep')
+    me = ep * TP + tp
+
+    def peer(mask):
+        return (flip_mask(tp, mask & 3), flip_mask(ep, mask >> 2))
+
+    pieces = [(c, i) for i in range(PER_CHUNK) for c in range(CHUNKS)]
+    loads = []
+    for n, (c, i) in enumerate(pieces):
+        rows = pl.ds(BLK * i, BLK)
+        keep, first = (keep0, keep1)[c], (first0, first1)[c]
+        loads.append([pltpu.make_async_copy(src, dst.at[n], load_sem.at[m, n]) for m, (src, dst) in enumerate((
+            (keep.at[1, rows], k1), (first.at[1, rows], f1), (keep.at[0, rows], k0), (first.at[0, rows], f0)))])
+    for group in (slice(0, 2), slice(2, 4)):
+        for load in loads:
+            for copy in load[group]:
+                copy.start()
+    x_load = pltpu.make_async_copy(all_hbm.at[:, pl.ds(0, TOK), :], xa, x_sem)
+    x_load.start()
+
+    barrier = pltpu.get_barrier_semaphore()
+    for mask in range(1, NDEV):
+        pl.semaphore_signal(barrier, inc=1, device_id=peer(mask), device_id_type=MESH)
+    pl.semaphore_wait(barrier, NDEV - 1)
+
+    sent = []
+
+    def send(src, dst, sems, at, mask):
+        copy = pltpu.make_async_remote_copy(src_ref=src, dst_ref=dst, send_sem=sems[0].at[at], recv_sem=sems[1].at[at],
+                                            device_id=peer(mask), device_id_type=MESH)
+        copy.start()
+        sent.append(copy)
+
+    def arrived(dst, sems, at):
+        pltpu.make_async_remote_copy(src_ref=dst, dst_ref=dst, send_sem=sems[0].at[at], recv_sem=sems[1].at[at],
+                                     device_id=peer(BIT_C), device_id_type=MESH).wait_recv()
+
+    for mask in range(1, NDEV):
+        send(o_ref.at[flip_mask(me, mask)], o_in.at[me], (o_send, o_recv), mask, mask)
+    o_own = pltpu.make_async_copy(o_ref.at[me], o_in.at[me], local_sem)
+    o_own.start()
+
+    def second_stage(n):
+        loads[n][0].wait()
+        loads[n][1].wait()
+        snd[n] = k1[n] + f1[n]
+        send(snd.at[n], rcv.at[n], (s2_send, s2_recv), n, (BIT_Y, BIT_Z)[pieces[n][0]])
+
+    for n in range(4):
+        second_stage(n)
+
+    x = x_ref[...]
+    wr = wr_ref[...]
+    logits = dot(x, wr)
+    ex = jnp.exp(logits - jnp.max(logits, axis=-1, keepdims=True))
+    probs = ex / jnp.sum(ex, axis=-1, keepdims=True)
+    slots = EXPERTS * STRIP
+    spread = (lax.broadcasted_iota(jnp.int32, (EXPERTS, slots), 1) // STRIP == lax.broadcasted_iota(jnp.int32, (EXPERTS, slots), 0))
+    spread = jnp.where(spread, 1.0, 0.0).astype(BF)
+    mark = mark_ref[...]
+    hi, mid, low = split3(GATE_SCALE * probs)
+    gate = (dot(hi, spread) + dot(mid, spread) + dot(low, spread)) * mark
+    for mask in range(1, NDEV):
+        arrived(o_in.at[flip_mask(me, mask)], (o_send, o_recv), mask)
+    o_own.wait()
+    o_rows = o_in[...].reshape(slots, D)
+    hi, mid, low = split3(gate)
+    routed = dot(hi, o_rows) + dot(mid, o_rows) + dot(low, o_rows)
+    seen = dot_nt(gy_ref[...], o_rows) * mark
+    hi, mid, low = split3(seen)
+    d_scores = GATE_SCALE * (dot_nt(hi, spread) + dot_nt(mid, spread) + dot_nt(low, spread))
+    d_logits = probs * (d_scores - jnp.sum(probs * d_scores, axis=-1, keepdims=True))
+    dl[me] = jnp.concatenate([d_logits[:TOK // 2], d_logits[TOK // 2:]], axis=1)
+    for mask in range(1, NDEV):
+        send(dl.at[me], dl.at[me], (dl_send, dl_recv), mask, mask)
+    for n in range(4, len(pieces)):
+        second_stage(n)
+    hi, mid, low = split3(d_logits)
+    dx_router = dot_nt(hi, wr) + dot_nt(mid, wr) + dot_nt(low, wr)
+
+    def finish_piece(n):
+        c, i = pieces[n]
+        arrived(rcv.at[n], (s2_send, s2_recv), n)
+        loads[n][2].wait()
+        loads[n][3].wait()
+        own = k0[n] + f0[n] + rcv[n]
+        for s in range(EP):
+            rows = own[2 * CAP * s:2 * CAP * (s + 1)]
+            ret[s, n] = jnp.concatenate([rows, jnp.zeros((16 - 2 * CAP, D), F32)], axis=0).astype(BF)
+        for at, mask in enumerate((BIT_X, BIT_C, BIT_X | BIT_C)):
+            send(ret.at[flip_mask(ep, mask >> 2), n], ret_in.at[ep, n], (ret_send, ret_recv), (n, at), mask)
+        ret_in[ep, n] = ret[ep, n]
+        (s_rows, d_rows)[c][SH_ROWS * i:SH_ROWS * (i + 1), :] = own[PAIR_ROWS:]
+
+    for n in range(4):
+        finish_piece(n)
+    for mask in range(1, NDEV):
+        arrived(dl.at[flip_mask(me, mask)], (dl_send, dl_recv), mask)
+    x_load.wait()
+    total = jnp.zeros((EXPERTS, D), F32)
+    for half in range(2):
+        x_half = xa[:, TOK // 2 * half:TOK // 2 * (half + 1), :].reshape(NDEV * TOK // 2, D)
+        for part in split3(dl[...].reshape(NDEV * TOK // 2, 2 * EXPERTS)):
+            total = total + dot_tn(part, x_half)[EXPERTS * half:EXPERTS * (half + 1)]
+    drt_ref[...] = total
+    for n in range(4, len(pieces)):
+        finish_piece(n)
+    y_ref[...] = (s_rows[...] + routed).astype(BF)
+    for n in range(len(pieces)):
+        for at, mask in enumerate((BIT_X, BIT_C, BIT_X | BIT_C)):
+            arrived(ret_in.at[flip_mask(ep, mask >> 2), n], (ret_send, ret_recv), (n, at))
+    back = ret_in[...].reshape(EP * STEPS * 16, D)
+    dx_ref[...] = (dx_router + d_rows[...] + dot(mark16_ref[...], back)).astype(BF)
+    for copy in sent:
+        copy.wait_send()
+
+
+def finish_call(keeps, firsts, o_send, x, grad_y, w_router, mark, mark16, all_rows):
+    vmem = pl.BlockSpec(memory_space=pltpu.VMEM)
+    anys = pl.BlockSpec(memory_space=pl.ANY)
+    pieces = PER_CHUNK * CHUNKS
+    piece = pltpu.VMEM((pieces, BLK, D), F32)
+    ret = pltpu.VMEM((EP, pieces, 16, D), BF)
+    dma = pltpu.SemaphoreType.DMA
+    return pl.pallas_call(
+        finish_kernel,
+        name='finish_call',
+        out_shape=(jax.ShapeDtypeStruct((TOK, D), BF), jax.ShapeDtypeStruct((TOK, D), BF), jax.ShapeDtypeStruct((EXPERTS, D), F32)),
+        in_specs=[anys] * 4 + [vmem] * 6 + [anys],
+        out_specs=(vmem, vmem, vmem),
+        scratch_shapes=[piece] * 6 + [ret, ret, pltpu.VMEM((NDEV, LOCAL // TP * STRIP, D), BF), pltpu.VMEM((NDEV, TOK // 2, 2 * EXPERTS), F32),
+                                      pltpu.VMEM((NDEV, TOK, D), BF), pltpu.VMEM((TOK, D), F32), pltpu.VMEM((TOK, D), F32),
+                                      dma((4, pieces)), dma, dma((pieces,)), dma((pieces,)), dma((pieces, 3)), dma((pieces, 3)),
+                                      dma((NDEV,)), dma((NDEV,)), dma((NDEV,)), dma((NDEV,)), dma],
+        compiler_params=pltpu.CompilerParams(collective_id=1, has_side_effects=True, vmem_limit_bytes=48 << 20),
+        cost_estimate=pl.CostEstimate(flops=50_000_000_000, bytes_accessed=20_000_000, transcendentals=0),
+    )(*keeps, *firsts, o_send, x, grad_y, w_router, mark, mark16, all_rows)
+
+
+def permutations(tp):
     row = jnp.arange(TP * PAIR_ROWS)
-    col, rest = row // PAIR_ROWS, row % PAIR_ROWS
+    col, rest = (row // PAIR_ROWS) ^ tp, row % PAIR_ROWS
     src, rest = rest // (2 * CAP), rest % (2 * CAP)
     which, slot = rest // CAP, rest % CAP
     wanted = col * (EP * STRIP) + src * STRIP + slot
@@ -341,15 +533,10 @@
 
 
 def solution(mesh):
-    def device_step(x, grad_y, w_router, w_gate, w_up, w_down, ws_gate, ws_up, ws_down, topk_idx):
+    def device_body(x, grad_y, w_router, w_gate, w_up, w_down, ws_gate, ws_up, ws_down, topk_idx):
         tp = lax.axis_index('tp')
         ep = lax.axis_index('ep')
         per = LOCAL // TP
-        w_down_in = []
-        for m in range(1, TP):
-            away = lax.dynamic_slice_in_dim(w_down, (tp ^ m) * per, per, axis=0)
-            w_down_in.append(lax.ppermute(away, 'tp', [(s, s ^ m) for s in range(TP)]))
-
         ids = jnp.arange(EXPERTS, dtype=jnp.int32)
         hit = jnp.any(topk_idx[:, :, None] == ids[None, None, :], axis=1)
         before = jnp.tril(jnp.ones((TOK, TOK), BF), -1)
@@ -359,20 +546,22 @@
         token = jnp.arange(TOK, dtype=jnp.int32)[:, None, None] + 1
         table = jnp.sum(jnp.where(slot_hit, token, 0), axis=0, dtype=jnp.int32) - 1
         table = jnp.concatenate([table.reshape(EP, LOCAL * STRIP), jnp.zeros((8 - EP, LOCAL * STRIP), jnp.int32)], axis=0)
-        all_rows, tables = gather_rows(jnp.concatenate([x, grad_y], axis=0), table)
+        rows_near, tables, w_early, all_rows = gather_rows(jnp.concatenate([x, grad_y], axis=0), table, w_down)
         mine = lax.dynamic_index_in_dim(tables, ep, 1, keepdims=False).reshape(EP, TP, LOCAL, STRIP)
+        w_late = []
+        for m in range(1, TP):
+            away = lax.dynamic_slice_in_dim(w_down, (tp ^ m) * per + EARLY, per - EARLY, axis=0)
+            w_late.append(lax.ppermute(away, 'tp', [(s, s ^ m) for s in range(TP)]))
         base = (TOK * jnp.arange(EP, dtype=jnp.int32))[:, None, None, None]
         slots = jnp.where(mine >= 0, mine + base, -1).transpose(1, 2, 0, 3).reshape(TP, LOCAL * EP * STRIP, 1)
 
-        parts, h, dab, xe, de = main_call(ep.reshape(1), all_rows, slots, w_router, ws_gate, ws_up, ws_down, permutations(), w_gate, w_up, w_down)
-        summed = lax.psum_scatter(parts, 'tp', scatter_dimension=0).reshape(STEPS, BLK, D)
-
+        *parts, h, dab, xe, de = main_call(jnp.stack([ep, tp]), rows_near, slots, w_router, ws_gate, ws_up, ws_down, permutations(tp), w_gate, w_up, w_down)
         h_in = []
         for m in range(1, TP):
             away = lax.dynamic_slice_in_dim(h, (tp ^ m) * per, per, axis=0)
             h_in.append(lax.ppermute(away, 'tp', [(s, s ^ m) for s in range(TP)]))
-        o_send = out_call(tp.reshape(1), h, h_in, w_down, w_down_in)
-        o_rows = lax.all_to_all(o_send, ('ep', 'tp'), 0, 0).reshape(EXPERTS * STRIP, D)
+        firsts = [lax.ppermute(parts[2 * c + 1], 'tp', [(s, s ^ (2 - c)) for s in range(TP)]) for c in range(CHUNKS)]
+        o_send = out_call(tp.reshape(1), h, h_in, w_down, w_early, w_late)
 
         d_w_gate, d_w_up, d_w_down = grad_call(xe, de, h, dab)
 
@@ -386,28 +575,14 @@
         ds_up = dot_tn(x_all, s_db)
         ds_down = dot_tn(s_h, gy_all)
 
-        probs = jax.nn.softmax(dot(x, w_router), axis=-1)
-        scaled = GATE_SCALE * probs
-        gate_slot = jnp.where(slot_hit, scaled[:, :, None], 0.0).reshape(TOK, EXPERTS * STRIP)
-        routed = jnp.dot(gate_slot, o_rows.astype(F32), precision=lax.Precision.HIGHEST)
-        seen = dot_nt(grad_y, o_rows).reshape(TOK, EXPERTS, STRIP)
-        d_scores = GATE_SCALE * jnp.sum(jnp.where(slot_hit, seen, 0.0), axis=2)
-        d_logits = probs * (d_scores - jnp.sum(probs * d_scores, axis=-1, keepdims=True))
-        d_logits_all = lax.all_gather(d_logits, ('ep', 'tp'), axis=0, tiled=True)
-        d_router = lax.dot_general(x_all.astype(F32), d_logits_all, (((0,), (0,)), ((), ())), precision=lax.Precision.HIGHEST)
-        dx_router = lax.dot_general(d_logits, w_router.astype(F32), (((1,), (1,)), ((), ())), precision=lax.Precision.HIGHEST)
-
-        half = STEPS // 2
-        shared = summed[:half, PAIR_ROWS:].reshape(TOK, D)
-        dx_shared = summed[half:, PAIR_ROWS:].reshape(TOK, D)
-        y_out = (shared + routed).astype(BF)
-        own = summed[:, :PAIR_ROWS].astype(BF).reshape(STEPS, EP, 2 * CAP, D).transpose(1, 0, 2, 3)
-        back = lax.all_to_all(own, 'ep', 0, 0).reshape(EXPERTS * CAP, D)
-        mark = slot_hit[:, :, :CAP].reshape(TOK, EXPERTS * CAP).astype(BF)
-        dx_out = (dx_router + dx_shared + dot(mark, back)).astype(BF)
+        mark = slot_hit.reshape(TOK, EXPERTS * STRIP).astype(F32)
+        mark16 = slot_hit[:, :, :CAP].reshape(TOK, EP, CHUNKS, PER_CHUNK, 2 * CAP).transpose(0, 1, 3, 2, 4)
+        mark16 = jnp.pad(mark16, ((0, 0),) * 4 + ((0, 16 - 2 * CAP),)).reshape(TOK, EP * STEPS * 16).astype(BF)
+        y_out, dx_out, d_router = finish_call(parts[0::2], firsts, o_send, x, grad_y, w_router, mark, mark16, all_rows)
+        d_router = d_router.T
         return y_out, dx_out, d_router, d_w_gate, d_w_up, d_w_down, ds_gate, ds_up, ds_down
 
     tok_spec = P(('ep', 'tp'), None)
     in_specs = (tok_spec, tok_spec, P(None, None), P('ep', None, 'tp'), P('ep', None, 'tp'), P('ep', 'tp', None), P(None, 'tp'), P(None, 'tp'), P('tp', None), tok_spec)
     out_specs = (tok_spec, tok_spec, P(None, None), P('ep', None, 'tp'), P('ep', None, 'tp'), P('ep', 'tp', None), P(None, 'tp'), P(None, 'tp'), P('tp', None))
-    return jax.shard_map(device_step, mesh=mesh, in_specs=in_specs, out_specs=out_specs, check_vma=False)
+    return jax.shard_map(device_body, mesh=mesh, in_specs=in_specs, out_specs=out_specs, check_vma=False)

time: 333 us -> 303 us (0.910)
  Pallas kernels: 77.4 us -> 181 us
  waiting for transfers between devices: 143 us -> 71 us
  blocking collectives: 27.8 us -> 0 us
  between operations: 14.4 us -> 1.12 us
  matrix products: 22.5 us -> 13.7 us
  local copies, waits for them, and re-layouts: 27.8 us -> 21.2 us
  starting transfers between devices: 14.4 us -> 9.01 us
    pallas_call x0 -> x1, Pallas kernels: none -> 69.6 us  [finish_call(): pl.pallas_call(finish_kernel, name='finish_call', out_shape=(jax.ShapeDty...]
    ppermute x6 -> x8, waiting for transfers between devices: 128 us -> 71 us  [the longest x3 70.9 us: device_body(): w_late.append(lax.ppermute(away, 'tp', [(s, s ^ m) for s in range(TP)]))]
    pallas_call x1, Pallas kernels: 27.8 us -> 63.3 us  [gather_rows(): pl.pallas_call(gather_kernel, name='gather_rows', out_shape=(jax.ShapeDty...]
    all_gather x1 -> x0, blocking collectives: 27.8 us -> none  [device_step(): d_logits_all = lax.all_gather(d_logits, ('ep', 'tp'), axis=0, tiled=True)]
    all_to_all x2 -> x0, waiting for transfers between devices: 11.9 us -> none  [the longest x1 8.98 us: device_step(): back = lax.all_to_all(own, 'ep', 0, 0).reshape(EXPERTS * CAP, D)]
    dot_general x3 -> x0, matrix products: 7.28 us -> none  [the longest x1 4.47 us: device_step(): lax.dot_general(x_all.astype(F32), d_logits_all, (((0,), (0,)), ((), ()))...]
    all_to_all x2 -> x0, starting transfers between devices: 6.21 us -> none  [the longest x1 3.76 us: device_step(): back = lax.all_to_all(own, 'ep', 0, 0).reshape(EXPERTS * CAP, D)]
    unnamed x41 -> x52, local copies, waits for them, and re-layouts: 14 us -> 11.2 us
  transfers between devices with their start and end apart: 9 -> 8, of which waited for: 5 -> 3; matrix products, arithmetic and copies ran while one was open for 9% -> 8% of each run, Pallas kernels for 6% -> 6%
where the time goes in v2:
time: 303 us; the launch traced here: 302 us
  Pallas kernels  181 us (60%)
  waiting for transfers between devices  71 us (23%)
  local copies, waits for them, and re-layouts  21.2 us (7%)
  matrix products  13.7 us (5%)
  starting transfers between devices  9.01 us (3%)
  other arithmetic  4.81 us (2%)
    ppermute x3, waiting for transfers between devices, device_body(): w_late.append(lax.ppermute(away, 'tp', [(s, s ^ m) for s in range(TP)]))  70.9 us
    pallas_call x1, Pallas kernels, finish_call(): pl.pallas_call(finish_kernel, name='finish_call', out_shape=(jax.ShapeDty...  69.6 us
    pallas_call x1, Pallas kernels, gather_rows(): pl.pallas_call(gather_kernel, name='gather_rows', out_shape=(jax.ShapeDty...  63.3 us
    pallas_call x1, Pallas kernels, main_call(): pl.pallas_call(main_kernel, name='main_call', grid_spec=pltpu.PrefetchSca...  29.8 us
    pallas_call x1, Pallas kernels, grad_call(): pl.pallas_call(grad_kernel, name='grad_call', grid=(LOCAL,), in_specs=[on...  15.6 us
    unnamed x52, local copies, waits for them, and re-layouts  11.2 us
    dot_general x3, matrix products, dot_tn(): lax.dot_general(a, b, (((0,), (0,)), ((), ())), preferred_element_type=F32)  6.85 us
  transfers between devices with their start and end apart: 8, of which 3 were waited for; matrix products, arithmetic and copies ran while one was open for 8% of the time, Pallas kernels for 6%

profile of v2, /device:TPU:0, one launch (start us, length us, event | category | flops | bytes accessed | tf_op | source)
XLA Modules:
  0.0 302.0 jit_solution(13865279199360332257)
XLA Ops:
  1.9 1.7 broadcast_bitcast_fusion
  5.9 63.3 %gather_rows.1 = (bf16[16,128,1536]{2,1,0:T(8,128)(2,1)S(1)}, s32[16,8,128]{2,1,0:T(8,128)S(1)}, bf16[3,2,128,1536]{3,2,1,0:T(8,128)(2,1)S(1)}, bf16[16,128,1536]{2,1,0:T(8,128)(2,1)}) custom-call(bf16[128,1536]{1,0:T(8,128)(2,1)S(1)} %pad_maximum_fusion.rows_ref, s32[8,128]{1,0:T(8,128)S(1)} %concatenate.7.tab_ref, bf16[16,128,1536]{2,1,0:T(8,128)(2,1)} %w_own.1), custom_call_target="tpu_custom_call" | custom-call | flops 40000000000 | bytes 7000000 | tf_op jit(solution)/shard_map/gather_rows/pallas_call | solution.py:170
  69.2 1.4 copy-done.6
  70.6 2.7 copy-done.8
  75.4 29.8 %main_call.1 = (f32[2,288,1536]{2,1,0:T(8,128)}, f32[2,288,1536]{2,1,0:T(8,128)}, f32[2,288,1536]{2,1,0:T(8,128)}, f32[2,288,1536]{2,1,0:T(8,128)}, bf16[16,128,...) custom-call(s32[2]{0:T(128)S(1)} %pad_add_fusion.g_ref, ...), custom_call_target="tpu_custom_call" | custom-call | flops 20000000000 | bytes 60000000 | tf_op jit(solution)/shard_map/main_call/pallas_call | solution.py:286
  107.0 1.4 collective-permute-start.4
  108.4 1.5 collective-permute-start.3
  110.5 1.5 collective-permute-start
  113.3 5.1 %fusion.36 = (bf16[16,64,1536]{2,1,0:T(8,128)(2,1)}, bf16[16,64,1536]{2,1,0:T(8,128)(2,1)S(1)}) fusion(bf16[16,128,1536]{2,1,0:T(8,128)(2,1)} %get-tuple-element.35.all_hbm), kind=kLoop, calls=%fused_computation.78 | loop fusion | bytes 12582912 | tf_op jit(solution)/shard_map/slice | solution.py:569
  118.4 1.8 convolution_convert_fusion
  120.2 1.8 convolution_convert_fusion.1
  122.1 3.1 %constant_dynamic-slice_fusion = (bf16[2,128,1536]{2,1,0:T(8,128)(2,1)}, bf16[2,128,1536]{2,1,0:T(8,128)(2,1)}, bf16[2,128,1536]{2,1,0:T(8,128)(2,1)S(1)}) fusion(bf16[16,128,1536]{2,1,0:T(8,128)(2,1)} %w_own.1, s32[]{:T(128)S(6)} %select_n.131, s32[]{:T(128)S(6)} %select_n.130, s32[]{:T(128)S(6)} %select_n.129), kind=kLoop, calls=%fused_computation.53 | loop fusion | bytes 4718604 | tf_op jit(solution)/shard_map/dynamic_slice | solution.py:553
  125.6 3.0 %convolution_convert_fusion.2 = bf16[1024,256]{1,0:T(8,128)(2,1)S(1)} fusion(bf16[1024,1536]{1,0:T(8,128)(2,1)} %bitcast.35, bf16[256,1536]{1,0:T(8,128)(2,1)S(1)} %copy-done.5), kind=kOutput, calls=%fused_computation.8 | convolution fusion | flops 805568512 | bytes 4456448 | tf_op jit(solution)/shard_map/dot_general | solution.py:51
  128.7 2.2 fusion.12
  130.9 2.3 fusion.14
  133.2 2.4 fusion.10
  135.6 1.5 collective-permute-start.7
  137.1 1.5 collective-permute-start.6
  139.2 15.6 %grad_call.1 = (f32[16,1536,128]{2,1,0:T(8,128)}, f32[16,1536,128]{2,1,0:T(8,128)}, f32[16,128,1536]{2,1,0:T(8,128)}) custom-call(bf16[16,128,1536]{2,1,0:T(8,128)(2,1)S(1)} %bitcast.28, bf16[16,128,1536]{2,1,0:T(8,128)(2,1)S(1)} %bitcast.30, bf16[16,128,128]{2,1,0:T(8,128)(2,1)S(1)} %get-tuple-element.33.h0.h_ref, bf16[16,128,256]{2,1,0:T(8,128)(2,1)S(1)} %copy-done.10), custom_call_target="tpu_custom_call" | custom-call | flops 10000000000 | bytes 55000000 | tf_op jit(solution)/shard_map/grad_call/pallas_call | solution.py:323
  154.8 55.2 %collective-permute-done.7.l3 = bf16[2,128,1536]{2,1,0:T(8,128)(2,1)S(1)} collective-permute-done((bf16[2,128,1536]{2,1,0:T(8,128)(2,1)}, bf16[2,128,1536]{2,1,0:T(8,128)(2,1)S(1)}, u32[]{:S(2)}, u32[]{:S(2)}) %collective-permute-start.7) | collective-permute-done | bytes 786464 | tf_op jit(solution)/shard_map/ppermute | solution.py:554
  210.0 15.6 %collective-permute-done.6.l2 = bf16[2,128,1536]{2,1,0:T(8,128)(2,1)S(1)} collective-permute-done((bf16[2,128,1536]{2,1,0:T(8,128)(2,1)}, bf16[2,128,1536]{2,1,0:T(8,128)(2,1)S(1)}, u32[]{:S(2)}, u32[]{:S(2)}) %collective-permute-start.6) | collective-permute-done | bytes 786464 | tf_op jit(solution)/shard_map/ppermute | solution.py:554
  225.7 1.7 copy-done.7
  227.4 2.8 out_call.1.o_ref
  230.3 69.6 %finish_call.1 = (bf16[64,1536]{1,0:T(8,128)(2,1)S(1)}, bf16[64,1536]{1,0:T(8,128)(2,1)S(1)}, f32[64,1536]{1,0:T(8,128)S(1)}) custom-call(f32[2,288,1536]{2,1,0:T(8,128)} %get-tuple-element.29.keep0, f32[2,288,1536]{2,1,0:T(8,128)} %get-tuple-element.30.keep1, f32[2,288,1536]{2,1,0:T(8,128)} %collective-permute-done.first0, ...), custom_call_target="tpu_custom_call" | custom-call | flops 49999998976 | bytes 20000000 | tf_op jit(solution)/shard_map/finish_call/pallas_call | solution.py:510
  (91 shorter events, 12.4 us)
Async XLA Ops:
  5.9 68.4 %copy-start.2 = (bf16[1536,256]{1,0:T(8,128)(2,1)S(1)}, bf16[1536,256]{1,0:T(8,128)(2,1)}, u32[]{:S(2)}) copy-start(bf16[1536,256]{1,0:T(8,128)(2,1)} %wsg_ref.1) | copy-start | bytes 2359300
  5.9 68.4 %copy-start.3 = (bf16[1536,256]{1,0:T(8,128)(2,1)S(1)}, bf16[1536,256]{1,0:T(8,128)(2,1)}, u32[]{:S(2)}) copy-start(bf16[1536,256]{1,0:T(8,128)(2,1)} %wsu_ref.1) | copy-start | bytes 2359300
  107.0 28.6 %collective-permute-start.4 = (bf16[4,128,128]{2,1,0:T(8,128)(2,1)}, bf16[4,128,128]{2,1,0:T(8,128)(2,1)S(1)}, u32[]{:S(2)}, u32[]{:S(2)}) collective-permute-start(bf16[4,128,128]{2,1,0:T(8,128)(2,1)} %get-tuple-element.50), channel_id=1, source_target_pairs={{0,12},{4,8},{8,4},{12,0},{1,13},{5,9},{9,5},{13,1},{2,14},{6,10},... | collective-permute-start | bytes 393224 | tf_op jit(solution)/shard_map/ppermute | solution.py:562
  108.4 28.7 %collective-permute-start.3 = (bf16[4,128,128]{2,1,0:T(8,128)(2,1)}, bf16[4,128,128]{2,1,0:T(8,128)(2,1)}, u32[]{:S(2)}, u32[]{:S(2)}) collective-permute-start(bf16[4,128,128]{2,1,0:T(8,128)(2,1)} %get-tuple-element.51), channel_id=1, source_target_pairs={{0,8},{4,12},{8,0},{12,4},{1,9},{5,13},{9,1},{13,5},{2,10},{6,14},... | collective-permute-start | bytes 393224 | tf_op jit(solution)/shard_map/ppermute | solution.py:562
  109.9 28.6 %collective-permute-start.2 = (bf16[4,128,128]{2,1,0:T(8,128)(2,1)}, bf16[4,128,128]{2,1,0:T(8,128)(2,1)}, u32[]{:S(2)}, u32[]{:S(2)}) collective-permute-start(bf16[4,128,128]{2,1,0:T(8,128)(2,1)} %get-tuple-element.52), channel_id=1, source_target_pairs={{0,4},{4,0},{8,12},{12,8},{1,5},{5,1},{9,13},{13,9},{2,6},{6,2},{1... | collective-permute-start | bytes 393224 | tf_op jit(solution)/shard_map/ppermute | solution.py:562
  110.5 119.8 %collective-permute-start = (f32[2,288,1536]{2,1,0:T(8,128)}, f32[2,288,1536]{2,1,0:T(8,128)}, u32[]{:S(2)}, u32[]{:S(2)}) collective-permute-start(f32[2,288,1536]{2,1,0:T(8,128)} %get-tuple-element.31), channel_id=1, source_target_pairs={{0,8},{4,12},{8,0},{12,4},{1,9},{5,13},{9,1},{13,5},{2,10},{6,14},... | collective-permute-start | bytes 10616840 | tf_op jit(solution)/shard_map/ppermute | solution.py:563
  111.9 118.3 %collective-permute-start.1 = (f32[2,288,1536]{2,1,0:T(8,128)}, f32[2,288,1536]{2,1,0:T(8,128)}, u32[]{:S(2)}, u32[]{:S(2)}) collective-permute-start(f32[2,288,1536]{2,1,0:T(8,128)} %get-tuple-element.32), channel_id=1, source_target_pairs={{0,4},{4,0},{8,12},{12,8},{1,5},{5,1},{9,13},{13,9},{2,6},{6,2},{1... | collective-permute-start | bytes 10616840 | tf_op jit(solution)/shard_map/ppermute | solution.py:563
  122.0 3.4 %copy-start.14 = (s32[64,512]{0,1:T(8,128)S(1)}, s32[64,512]{0,1:T(8,128)}, u32[]{:S(2)}) copy-start(s32[64,512]{0,1:T(8,128)} %get-tuple-element.53) | copy-start | bytes 393220
  122.0 3.6 %copy-start.5 = (bf16[256,1536]{1,0:T(8,128)(2,1)S(1)}, bf16[256,1536]{1,0:T(8,128)(2,1)}, u32[]{:S(2)}) copy-start(bf16[256,1536]{1,0:T(8,128)(2,1)} %wsd_ref.1) | copy-start | bytes 2359300
  125.5 3.1 %copy-start.13 = (bf16[16,64,1536]{2,1,0:T(8,128)(2,1)S(1)}, bf16[16,64,1536]{2,1,0:T(8,128)(2,1)}, u32[]{:S(2)}) copy-start(bf16[16,64,1536]{2,1,0:T(8,128)(2,1)} %get-tuple-element.45) | copy-start | bytes 9437188
  125.6 3.1 %copy-start.16 = (bf16[1024,256]{1,0:T(8,128)(2,1)S(1)}, bf16[1024,256]{1,0:T(8,128)(2,1)}, u32[]{:S(2)}) copy-start(bf16[1024,256]{1,0:T(8,128)(2,1)} %convolution_convert_fusion) | copy-start | bytes 1572868
  125.6 3.1 %copy-start.17 = (bf16[1024,256]{1,0:T(8,128)(2,1)S(1)}, bf16[1024,256]{1,0:T(8,128)(2,1)}, u32[]{:S(2)}) copy-start(bf16[1024,256]{1,0:T(8,128)(2,1)} %convolution_convert_fusion.1) | copy-start | bytes 1572868
  128.7 10.4 %slice-start.4 = ((s8[6291456]{0:T(1024)(128)(4,1)}), s8[4194304]{0:T(1024)(128)(4,1)S(1)}, s32[]{:S(2)}) async-start(s8[6291456]{0:T(1024)(128)(4,1)} %bitcast.29), calls=%async_computation.4 | async-start | bytes 8388608
  130.9 8.2 %slice-start.2 = ((s8[6291456]{0:T(1024)(128)(4,1)}), s8[4194304]{0:T(1024)(128)(4,1)S(1)}, s32[]{:S(2)}) async-start(s8[6291456]{0:T(1024)(128)(4,1)} %bitcast.27), calls=%async_computation.2 | async-start | bytes 8388608
  130.9 8.2 %slice-start.5 = ((s8[6291456]{0:T(1024)(128)(4,1)}), s8[2097152]{0:T(1024)(128)(4,1)S(1)}, s32[]{:S(2)}) async-start(s8[6291456]{0:T(1024)(128)(4,1)} %bitcast.29), calls=%async_computation.5 | async-start | bytes 4194304
  133.2 6.0 %slice-start.3 = ((s8[6291456]{0:T(1024)(128)(4,1)}), s8[2097152]{0:T(1024)(128)(4,1)S(1)}, s32[]{:S(2)}) async-start(s8[6291456]{0:T(1024)(128)(4,1)} %bitcast.27), calls=%async_computation.3 | async-start | bytes 4194304
  133.2 6.0 %copy-start.10 = (bf16[16,128,256]{2,1,0:T(8,128)(2,1)S(1)}, bf16[16,128,256]{2,1,0:T(8,128)(2,1)}, u32[]{:S(2)}) copy-start(bf16[16,128,256]{2,1,0:T(8,128)(2,1)} %copy-done.9) | copy-start | bytes 3145732
  133.2 92.6 %slice-start = ((s8[6291456]{0:T(1024)(128)(4,1)}), s8[4194304]{0:T(1024)(128)(4,1)S(1)}, s32[]{:S(2)}) async-start(s8[6291456]{0:T(1024)(128)(4,1)} %bitcast.24), calls=%async_computation | async-start | bytes 8388608
  135.6 74.4 %collective-permute-start.7 = (bf16[2,128,1536]{2,1,0:T(8,128)(2,1)}, bf16[2,128,1536]{2,1,0:T(8,128)(2,1)S(1)}, u32[]{:S(2)}, u32[]{:S(2)}) collective-permute-start(bf16[2,128,1536]{2,1,0:T(8,128)(2,1)} %get-tuple-element.47), channel_id=1, source_target_pairs={{0,12},{4,8},{8,4},{12,0},{1,13},{5,9},{9,5},{13,1},{2,14},{6,10},... | collective-permute-start | bytes 2359304 | tf_op jit(solution)/shard_map/ppermute | solution.py:554
  137.1 88.5 %collective-permute-start.6 = (bf16[2,128,1536]{2,1,0:T(8,128)(2,1)}, bf16[2,128,1536]{2,1,0:T(8,128)(2,1)S(1)}, u32[]{:S(2)}, u32[]{:S(2)}) collective-permute-start(bf16[2,128,1536]{2,1,0:T(8,128)(2,1)} %get-tuple-element.48), channel_id=1, source_target_pairs={{0,8},{4,12},{8,0},{12,4},{1,9},{5,13},{9,1},{13,5},{2,10},{6,14},... | collective-permute-start | bytes 2359304 | tf_op jit(solution)/shard_map/ppermute | solution.py:554
  138.6 87.2 %collective-permute-start.5 = (bf16[2,128,1536]{2,1,0:T(8,128)(2,1)S(1)}, bf16[2,128,1536]{2,1,0:T(8,128)(2,1)S(1)}, u32[]{:S(2)}, u32[]{:S(2)}) collective-permute-start(bf16[2,128,1536]{2,1,0:T(8,128)(2,1)S(1)} %get-tuple-element.49), channel_id=1, source_target_pairs={{0,4},{4,0},{8,12},{12,8},{1,5},{5,1},{9,13},{13,9},{2,6},{6,2},{1... | collective-permute-start | bytes 2359304 | tf_op jit(solution)/shard_map/ppermute | solution.py:554
  139.1 86.6 %slice-start.1 = ((s8[6291456]{0:T(1024)(128)(4,1)}), s8[2097152]{0:T(1024)(128)(4,1)S(1)}, s32[]{:S(2)}) async-start(s8[6291456]{0:T(1024)(128)(4,1)} %bitcast.24), calls=%async_computation.1 | async-start | bytes 4194304
  227.4 2.9 copy-start
  227.4 2.9 copy-start.1
  (8 other events, 13.6 us)

commit v3 on v2

--- a/solution.py
+++ b/solution.py
@@ -1,5 +1,6 @@
 import jax
 import jax.numpy as jnp
+import numpy as np
 from jax import lax
 from jax.experimental import pallas as pl
 from jax.experimental.pallas import tpu as pltpu
@@ -13,6 +14,7 @@
 
 D = 1536
 EXPERTS = 64
+TOP = 6
 TOK = 64
 TP = 4
 EP = 4
@@ -27,7 +29,6 @@
 BLK = PAIR_ROWS + SH_ROWS
 CHUNKS = 2
 PER_CHUNK = STEPS // CHUNKS
-EARLY = 2
 
 BIT_Y, BIT_Z, BIT_C, BIT_X = 1, 2, 4, 8
 
@@ -64,7 +65,7 @@
     return h, da, db
 
 
-def gather_kernel(rows_ref, tab_ref, w_ref, all_ref, tabs_ref, w_in_ref, keep_ref, send_sem, recv_sem, local_sem, w_send, w_recv, keep_sem):
+def gather_rows(x_ref, gy_ref, tab_ref, w_ref, all_ref, tabs_ref, w_in_ref, keep_ref, send_sem, recv_sem, local_sem, w_send, w_recv, keep_sem):
     tp = lax.axis_index('tp')
     ep = lax.axis_index('ep')
     me = ep * TP + tp
@@ -73,43 +74,40 @@
     def peer(mask):
         return (flip_mask(tp, mask & 3), flip_mask(ep, mask >> 2))
 
+    own = [pltpu.make_async_copy(x_ref, all_ref.at[me, pl.ds(0, TOK)], local_sem.at[0]),
+           pltpu.make_async_copy(gy_ref, all_ref.at[me, pl.ds(TOK, TOK)], local_sem.at[1]),
+           pltpu.make_async_copy(tab_ref, tabs_ref.at[me], local_sem.at[2])]
+    for c in own:
+        c.start()
     barrier = pltpu.get_barrier_semaphore()
     for mask in (BIT_X, BIT_Y, BIT_Z, BIT_C, BIT_Y | BIT_Z):
         pl.semaphore_signal(barrier, inc=1, device_id=peer(mask), device_id_type=MESH)
     pl.semaphore_wait(barrier, 5)
+    for c in own:
+        c.wait()
+
+    orders = [(BIT_Y, BIT_Z, BIT_X), (BIT_Z, BIT_Y, BIT_X), (BIT_Y, BIT_Z, BIT_X), (BIT_Z, BIT_Y, BIT_X)]
+
+    def view(part, block):
+        if part == 3:
+            return tabs_ref.at[block]
+        return all_ref.at[block, :, pl.ds(part * third, third)]
 
     sent = []
-    for m in range(1, TP):
-        first = flip_mask(tp, m) * (LOCAL // TP)
-        c = pltpu.make_async_remote_copy(src_ref=w_ref.at[pl.ds(first, EARLY)], dst_ref=w_in_ref.at[m - 1],
-                                         send_sem=w_send.at[m - 1], recv_sem=w_recv.at[m - 1], device_id=peer(m), device_id_type=MESH)
-        c.start()
-        sent.append(c)
-
-    orders = [(BIT_X, BIT_Y, BIT_Z), (BIT_Y, BIT_Z, BIT_X), (BIT_Z, BIT_X, BIT_Y), (BIT_X, BIT_Y, BIT_Z)]
-
-    def view(part, block, own):
-        if part == 3:
-            return tab_ref if own else tabs_ref.at[block]
-        cols = pl.ds(part * third, third)
-        return rows_ref.at[:, cols] if own else all_ref.at[block, :, cols]
-
-    def copy(part, k, mask):
+
+    def send(part, k, mask):
         block = flip_mask(me, k)
-        return pltpu.make_async_remote_copy(
-            src_ref=view(part, block, k == 0), dst_ref=view(part, block, False),
+        c = pltpu.make_async_remote_copy(
+            src_ref=view(part, block), dst_ref=view(part, block),
             send_sem=send_sem.at[part, k ^ mask], recv_sem=recv_sem.at[part, k ^ mask],
             device_id=peer(mask), device_id_type=MESH)
-
-    def send(part, k, mask):
-        c = copy(part, k, mask)
         c.start()
         sent.append(c)
 
     def arrived(part, k):
         block = flip_mask(me, k)
         pltpu.make_async_remote_copy(
-            src_ref=view(part, block, False), dst_ref=view(part, block, False),
+            src_ref=view(part, block), dst_ref=view(part, block),
             send_sem=send_sem.at[part, k], recv_sem=recv_sem.at[part, k],
             device_id=peer(BIT_C), device_id_type=MESH).wait_recv()
 
@@ -119,16 +117,17 @@
             send(part, 0, orders[part][step])
     for part in parts:
         send(part, 0, BIT_C)
-    own_rows = pltpu.make_async_copy(rows_ref, all_ref.at[me], local_sem.at[0])
-    own_tab = pltpu.make_async_copy(tab_ref, tabs_ref.at[me], local_sem.at[1])
-    own_rows.start()
-    own_tab.start()
     for part in parts:
         m1, m2, m3 = orders[part]
         arrived(part, m1)
         send(part, m1, m2)
         send(part, m1, m3)
         send(part, m1, BIT_C)
+    per = LOCAL // TP
+    for m in range(1, TP):
+        c = pltpu.make_async_remote_copy(src_ref=w_ref.at[pl.ds(flip_mask(tp, m) * per, per)], dst_ref=w_in_ref.at[m - 1],
+                                         send_sem=w_send.at[m - 1], recv_sem=w_recv.at[m - 1], device_id=peer(m), device_id_type=MESH)
+        c.start()
     for part in parts:
         m1, m2, m3 = orders[part]
         arrived(part, m2)
@@ -145,8 +144,6 @@
             k = (m3, m1 ^ m3, m2 ^ m3, m1 ^ m2 ^ m3)[extra]
             arrived(part, k)
             send(part, k, BIT_C)
-    own_rows.wait()
-    own_tab.wait()
     kept = []
     for k in sorted(range(16), key=lambda k: k & BIT_C):
         if k & BIT_C:
@@ -158,61 +155,66 @@
         kept.append(c)
     for c in kept:
         c.wait()
-    for c in sent[:TP - 1]:
-        c.wait_recv()
     for c in sent:
         c.wait_send()
 
 
-def gather_rows(rows, tab, w_down):
-    vmem = pl.BlockSpec(memory_space=pltpu.VMEM)
-    hbm = pl.BlockSpec(memory_space=pltpu.HBM)
-    return pl.pallas_call(
-        gather_kernel,
-        name='gather_rows',
-        out_shape=(jax.ShapeDtypeStruct((NDEV,) + rows.shape, rows.dtype), jax.ShapeDtypeStruct((NDEV,) + tab.shape, tab.dtype),
-                   jax.ShapeDtypeStruct((TP - 1, EARLY) + w_down.shape[1:], w_down.dtype), jax.ShapeDtypeStruct((NDEV,) + rows.shape, rows.dtype)),
-        in_specs=[vmem, vmem, hbm],
-        out_specs=(vmem, vmem, hbm, hbm),
-        scratch_shapes=[pltpu.SemaphoreType.DMA((4, 16)), pltpu.SemaphoreType.DMA((4, 16)), pltpu.SemaphoreType.DMA((2,)),
-                        pltpu.SemaphoreType.DMA((TP - 1,)), pltpu.SemaphoreType.DMA((TP - 1,)), pltpu.SemaphoreType.DMA((NDEV,))],
-        compiler_params=pltpu.CompilerParams(collective_id=0, has_side_effects=True, vmem_limit_bytes=40 << 20),
-        cost_estimate=pl.CostEstimate(flops=40_000_000_000, bytes_accessed=7_000_000, transcendentals=0),
-    )(rows, tab, w_down)
+def split3(v):
+    hi = v.astype(BF)
+    rest = v - hi.astype(F32)
+    mid = rest.astype(BF)
+    return hi, mid, (rest - mid.astype(F32)).astype(BF)
 
 
 def chunk_members(chunk):
     return ((0, 1), (2, 3)) if chunk % 2 == 0 else ((0, 2), (1, 3))
 
 
-def main_kernel(g_ref, all_ref, slot_ref, wr_ref, wsg_ref, wsu_ref, wsd_ref, perm_ref, wg_ref, wu_ref, wd_ref, *refs):
-    chunk_refs, (h_ref, dab_ref, xe_hbm, de_hbm, xe, de, sh, sems) = refs[:2 * CHUNKS], refs[2 * CHUNKS:]
+def main_kernel(x_ref, gy_ref, tab_ref, w_all_ref, wr_ref, wsg_ref, wsu_ref, wsd_ref, perm_ref, wg_ref, wu_ref, wd_ref, *refs):
+    chunk_refs, refs = refs[:2 * CHUNKS], refs[2 * CHUNKS:]
+    (h_ref, dab_ref, xe_hbm, de_hbm, w_in_ref, keep_ref, h_in_ref, all_ref, tabs_ref, xe, de, sh, hs, sems,
+     send_sem, recv_sem, local_sem, w_send, w_recv, keep_sem, h_send, h_recv) = refs
     step = pl.program_id(0)
-    g = g_ref[0]
-    tp = g_ref[1]
+    g = lax.axis_index('ep')
+    tp = lax.axis_index('tp')
     third = D // 3
+    per = LOCAL // TP
     xe_copy = pltpu.make_async_copy(xe, xe_hbm, sems.at[0])
     de_copy = pltpu.make_async_copy(de, de_hbm, sems.at[1])
 
     @pl.when(step == 0)
     def _():
+        gather_rows(x_ref, gy_ref, tab_ref, w_all_ref, all_ref, tabs_ref, w_in_ref, keep_ref, send_sem, recv_sem, local_sem, w_send, w_recv, keep_sem)
         n_rows = LOCAL * EP * STRIP
-        lane = lax.broadcasted_iota(jnp.int32, (n_rows, EP * TOK), 1)
+        expert = g * LOCAL + lax.broadcasted_iota(jnp.int32, (LOCAL, TOK), 0)
+        early = lax.broadcasted_iota(jnp.int32, (EP * TOK, EP * TOK), 0)
+        late = lax.broadcasted_iota(jnp.int32, (EP * TOK, EP * TOK), 1)
+        before = jnp.where((early < late) & (early // TOK == late // TOK), 1.0, 0.0).astype(BF)
+        cube = (LOCAL, EP * STRIP, EP * TOK)
+        place = lax.broadcasted_iota(jnp.int32, cube, 1)
+        wanted_rank = (place % STRIP).astype(F32)
+        same_source = place // STRIP == lax.broadcasted_iota(jnp.int32, cube, 2) // TOK
         wr = wr_ref[...]
         row_expert = g * LOCAL + lax.broadcasted_iota(jnp.int32, (n_rows, 3 * EXPERTS), 0) // (EP * STRIP)
         wanted = lax.broadcasted_iota(jnp.int32, (n_rows, 3 * EXPERTS), 1) % EXPERTS == row_expert
         for j in range(TP):
-            pick = jnp.where(slot_ref[j] == lane, 1.0, 0.0).astype(BF)
+            hit = []
+            for s in range(EP):
+                ids = tabs_ref[s * TP + j]
+                found = ids[0:1, :] == expert
+                for k in range(1, TOP):
+                    found = found | (ids[k:k + 1, :] == expert)
+                hit.append(jnp.where(found, 1.0, 0.0))
+            hit = jnp.concatenate(hit, axis=1)
+            rank = jnp.where(hit > 0.0, dot(hit.astype(BF), before), -1.0)
+            rank = jnp.broadcast_to(rank[:, None, :], cube)
+            pick = jnp.where((rank == wanted_rank) & same_source, 1.0, 0.0).reshape(n_rows, EP * TOK).astype(BF)
             x_j = jnp.concatenate([all_ref[s * TP + j, :TOK, :] for s in range(EP)], axis=0)
-            logits = dot(x_j, wr)
+            logits = dot_nt(x_j, wr)
             top = jnp.max(logits, axis=-1, keepdims=True)
             ex = jnp.exp(logits - top)
             probs = ex / jnp.sum(ex, axis=-1, keepdims=True)
-            hi = probs.astype(BF)
-            rest = probs - hi.astype(F32)
-            mid = rest.astype(BF)
-            low = (rest - mid.astype(F32)).astype(BF)
-            sel = dot(pick, jnp.concatenate([hi, mid, low], axis=1))
+            sel = dot(pick, jnp.concatenate(split3(probs), axis=1))
             gate = GATE_SCALE * jnp.sum(jnp.where(wanted, sel, 0.0), axis=1, keepdims=True)
             for n in range(3):
                 cols = slice(n * third, (n + 1) * third)
@@ -244,8 +246,10 @@
         width = ab.shape[1] // 2
         h, da, db = act_both(ab[:, :width], ab[:, width:], dh)
         h_ref[i] = h
+        hs[e] = h
         dab = jnp.concatenate([da, db], axis=1)
         dab_ref[i] = dab
+        dab = jnp.concatenate([dab_ref[i, pl.ds(pl.multiple_of(flip_mask(tp, rel) * EP * STRIP, EP * STRIP), EP * STRIP), :] for rel in range(TP)], axis=0)
         lhs.append(dot(perm_ref[i], dab).astype(BF))
     lhs = jnp.concatenate(lhs, axis=1)
     half = step // (STEPS // 2)
@@ -262,48 +266,65 @@
                 for at, rel in enumerate(members):
                     for n in range(3):
                         ref[at, :PAIR_ROWS, n * third:(n + 1) * third] = found[n][rel]
-                    away = rel ^ tp
+                    away = flip_mask(tp, rel)
                     ref[at, PAIR_ROWS:, :] = sh[half, away, pl.ds(first, SH_ROWS), :]
 
     @pl.when(step == STEPS - 1)
     def _():
+        h_copies = []
+        for m in range(1, TP):
+            to = flip_mask(tp, m)
+            c = pltpu.make_async_remote_copy(src_ref=hs.at[pl.ds(to * per, per)], dst_ref=h_in_ref.at[m - 1],
+                                             send_sem=h_send.at[m - 1], recv_sem=h_recv.at[m - 1], device_id=(to, g), device_id_type=MESH)
+            c.start()
+            h_copies.append(c)
         xe_copy.wait()
         de_copy.wait()
-
-
-def main_call(g, all_rows, slots, w_router, ws_gate, ws_up, ws_down, perm, w_gate, w_up, w_down):
+        for m in range(1, TP):
+            to = flip_mask(tp, m)
+            pltpu.make_async_remote_copy(src_ref=w_all_ref.at[pl.ds(to * per, per)], dst_ref=w_in_ref.at[m - 1],
+                                         send_sem=w_send.at[m - 1], recv_sem=w_recv.at[m - 1], device_id=(to, g), device_id_type=MESH).wait()
+        for c in h_copies:
+            c.wait()
+
+
+def main_call(x, grad_y, table, w_router, ws_gate, ws_up, ws_down, perm, w_gate, w_up, w_down):
     width = w_gate.shape[2]
+    per = LOCAL // TP
 
     def whole(a):
-        return pl.BlockSpec(a.shape, lambda i, g_: (0,) * a.ndim, pipeline_mode=pl.Buffered(1))
+        return pl.BlockSpec(a.shape, lambda i: (0,) * a.ndim, pipeline_mode=pl.Buffered(1))
 
     def pair(a):
-        return pl.BlockSpec((2,) + a.shape[1:], lambda i, g_: (i, 0, 0))
-
-    any_spec = pl.BlockSpec(memory_space=pl.ANY)
-    chunk_specs = [pl.BlockSpec((2, BLK, D), lambda i, g_, c=n // 2: (0, jnp.clip(i - PER_CHUNK * c, 0, PER_CHUNK - 1), 0))
+        return pl.BlockSpec((2,) + a.shape[1:], lambda i: (i, 0, 0))
+
+    hbm = pl.BlockSpec(memory_space=pltpu.HBM)
+    vmem = pl.BlockSpec(memory_space=pltpu.VMEM)
+    dma = pltpu.SemaphoreType.DMA
+    chunk_specs = [pl.BlockSpec((2, BLK, D), lambda i, c=n // 2: (0, jnp.clip(i - PER_CHUNK * c, 0, PER_CHUNK - 1), 0))
                    for n in range(2 * CHUNKS)]
     return pl.pallas_call(
         main_kernel,
         name='main_call',
-        grid_spec=pltpu.PrefetchScalarGridSpec(
-            num_scalar_prefetch=1,
-            grid=(STEPS,),
-            in_specs=[pl.BlockSpec(memory_space=pltpu.VMEM), whole(slots), whole(w_router), whole(ws_gate), whole(ws_up), whole(ws_down), whole(perm),
-                      pair(w_gate), pair(w_up), pair(w_down)],
-            out_specs=chunk_specs + [
-                       pl.BlockSpec((2, ROWS, width), lambda i, g_: (i, 0, 0)),
-                       pl.BlockSpec((2, ROWS, 2 * width), lambda i, g_: (i, 0, 0)), any_spec, any_spec],
-            scratch_shapes=[pltpu.VMEM((LOCAL, ROWS, D), BF), pltpu.VMEM((LOCAL, ROWS, D), BF),
-                            pltpu.VMEM((2, TP, TOK, D), F32), pltpu.SemaphoreType.DMA((2,))],
-        ),
+        grid=(STEPS,),
+        in_specs=[vmem, vmem, vmem, hbm, whole(w_router), whole(ws_gate), whole(ws_up), whole(ws_down), whole(perm),
+                  pair(w_gate), pair(w_up), pair(w_down)],
+        out_specs=chunk_specs + [
+            pl.BlockSpec((2, ROWS, width), lambda i: (i, 0, 0)),
+            pl.BlockSpec((2, ROWS, 2 * width), lambda i: (i, 0, 0)), hbm, hbm, hbm, hbm, hbm],
+        scratch_shapes=[pltpu.VMEM((NDEV, 2 * TOK, D), BF), pltpu.VMEM((NDEV,) + table.shape, jnp.int32),
+                        pltpu.VMEM((LOCAL, ROWS, D), BF), pltpu.VMEM((LOCAL, ROWS, D), BF),
+                        pltpu.VMEM((2, TP, TOK, D), F32), pltpu.VMEM((LOCAL, ROWS, width), BF), dma((2,)),
+                        dma((4, 16)), dma((4, 16)), dma((3,)), dma((TP - 1,)), dma((TP - 1,)), dma((NDEV,)), dma((TP - 1,)), dma((TP - 1,))],
         out_shape=[jax.ShapeDtypeStruct((2, BLK * PER_CHUNK, D), F32)] * (2 * CHUNKS) + [
-                   jax.ShapeDtypeStruct((LOCAL, ROWS, width), BF),
-                   jax.ShapeDtypeStruct((LOCAL, ROWS, 2 * width), BF),
-                   jax.ShapeDtypeStruct((LOCAL, ROWS, D), BF), jax.ShapeDtypeStruct((LOCAL, ROWS, D), BF)],
-        compiler_params=pltpu.CompilerParams(vmem_limit_bytes=48 << 20),
-        cost_estimate=pl.CostEstimate(flops=20_000_000_000, bytes_accessed=60_000_000, transcendentals=4_000_000),
-    )(g, all_rows, slots, w_router, ws_gate, ws_up, ws_down, perm, w_gate, w_up, w_down)
+            jax.ShapeDtypeStruct((LOCAL, ROWS, width), BF),
+            jax.ShapeDtypeStruct((LOCAL, ROWS, 2 * width), BF),
+            jax.ShapeDtypeStruct((LOCAL, ROWS, D), BF), jax.ShapeDtypeStruct((LOCAL, ROWS, D), BF),
+            jax.ShapeDtypeStruct((TP - 1, per) + w_down.shape[1:], BF), jax.ShapeDtypeStruct((NDEV, 2 * TOK, D), BF),
+            jax.ShapeDtypeStruct((TP - 1, per, ROWS, width), BF)],
+        compiler_params=pltpu.CompilerParams(collective_id=0, has_side_effects=True, vmem_limit_bytes=58 << 20),
+        cost_estimate=pl.CostEstimate(flops=60_000_000_000, bytes_accessed=60_000_000, transcendentals=4_000_000),
+    )(x, grad_y, table, w_down, w_router, ws_gate, ws_up, ws_down, perm, w_gate, w_up, w_down)
 
 
 def grad_kernel(xe_ref, de_ref, h_ref, dab_ref, dg_ref, du_ref, dd_ref):
@@ -333,49 +354,40 @@
     )(xe, de, h, dab)
 
 
-def out_kernel(tp_ref, h0, h1, h2, h3, w_own, e1, e2, e3, l1, l2, l3, o_ref):
-    def emit(e, w1, w2, w3):
-        total = dot(jnp.concatenate([h0[0], h1[0], h2[0], h3[0]], axis=1), jnp.concatenate([w_own[0], w1, w2, w3], axis=0))
-        for j in range(TP):
-            for s in range(EP):
-                first = STRIP * (j * EP + s)
-                o_ref[s * TP + j, STRIP * e:STRIP * (e + 1), :] = total[first:first + STRIP].astype(BF)
-
+def out_kernel(tp_ref, h0, h1, h2, h3, w0, w1, w2, w3, o_ref):
+    total = dot(jnp.concatenate([h0[0], h1[0, 0], h2[0, 0], h3[0, 0]], axis=1), jnp.concatenate([w0[0], w1[0, 0], w2[0, 0], w3[0, 0]], axis=0))
     for e in range(LOCAL // TP):
         @pl.when(pl.program_id(0) == e)
         def _(e=e):
-            if e < EARLY:
-                emit(e, e1[0, 0], e2[0, 0], e3[0, 0])
-            else:
-                emit(e, l1[0], l2[0], l3[0])
-
-
-def out_call(tp, h_own, h_in, w_down, w_early, w_late):
-    width = h_own.shape[2]
+            for j in range(TP):
+                for s in range(EP):
+                    first = STRIP * (j * EP + s)
+                    o_ref[s * TP + j, STRIP * e:STRIP * (e + 1), :] = total[first:first + STRIP].astype(BF)
+
+
+def out_call(tp, h, h_in, w, w_in):
+    width = h.shape[2]
     per = LOCAL // TP
+
+    def own(shape):
+        return pl.BlockSpec((1,) + shape, lambda i, t: (t[0] * per + i, 0, 0))
+
+    def got(shape):
+        return [pl.BlockSpec((1, 1) + shape, lambda i, t, m=m: (m, i, 0, 0)) for m in range(TP - 1)]
+
     return pl.pallas_call(
         out_kernel,
         name='out_call',
         grid_spec=pltpu.PrefetchScalarGridSpec(
             num_scalar_prefetch=1,
             grid=(per,),
-            in_specs=[pl.BlockSpec((1, ROWS, width), lambda i, t: (t[0] * per + i, 0, 0))] + [pl.BlockSpec((1, ROWS, width), lambda i, t: (i, 0, 0))] * 3
-            + [pl.BlockSpec((1, width, D), lambda i, t: (t[0] * per + i, 0, 0))]
-            + [pl.BlockSpec((1, 1, width, D), lambda i, t, m=m: (m, jnp.minimum(i, EARLY - 1), 0, 0)) for m in range(TP - 1)]
-            + [pl.BlockSpec((1, width, D), lambda i, t: (jnp.maximum(i - EARLY, 0), 0, 0))] * 3,
+            in_specs=[own((ROWS, width))] + got((ROWS, width)) + [own((width, D))] + got((width, D)),
             out_specs=pl.BlockSpec((NDEV, per * STRIP, D), lambda i, t: (0, 0, 0)),
         ),
         out_shape=jax.ShapeDtypeStruct((NDEV, per * STRIP, D), BF),
         compiler_params=pltpu.CompilerParams(vmem_limit_bytes=40 << 20),
         cost_estimate=pl.CostEstimate(flops=5_000_000_000, bytes_accessed=10_000_000, transcendentals=0),
-    )(tp, h_own, *h_in, w_down, w_early, w_early, w_early, *w_late)
-
-
-def split3(v):
-    hi = v.astype(BF)
-    rest = v - hi.astype(F32)
-    mid = rest.astype(BF)
-    return hi, mid, (rest - mid.astype(F32)).astype(BF)
+    )(tp, h, h_in, h_in, h_in, w, w_in, w_in, w_in)
 
 
 def finish_kernel(keep0, keep1, first0, first1, o_ref, x_ref, gy_ref, wr_ref, mark_ref, mark16_ref, all_hbm,
@@ -436,7 +448,7 @@
 
     x = x_ref[...]
     wr = wr_ref[...]
-    logits = dot(x, wr)
+    logits = dot_nt(x, wr)
     ex = jnp.exp(logits - jnp.max(logits, axis=-1, keepdims=True))
     probs = ex / jnp.sum(ex, axis=-1, keepdims=True)
     slots = EXPERTS * STRIP
@@ -461,7 +473,7 @@
     for n in range(4, len(pieces)):
         second_stage(n)
     hi, mid, low = split3(d_logits)
-    dx_router = dot_nt(hi, wr) + dot_nt(mid, wr) + dot_nt(low, wr)
+    dx_router = dot(hi, wr) + dot(mid, wr) + dot(low, wr)
 
     def finish_piece(n):
         c, i = pieces[n]
@@ -522,46 +534,28 @@
     )(*keeps, *firsts, o_send, x, grad_y, w_router, mark, mark16, all_rows)
 
 
-def permutations(tp):
-    row = jnp.arange(TP * PAIR_ROWS)
-    col, rest = (row // PAIR_ROWS) ^ tp, row % PAIR_ROWS
+def permutations():
+    row = np.arange(TP * PAIR_ROWS)
+    col, rest = row // PAIR_ROWS, row % PAIR_ROWS
     src, rest = rest // (2 * CAP), rest % (2 * CAP)
     which, slot = rest // CAP, rest % CAP
-    wanted = col * (EP * STRIP) + src * STRIP + slot
-    hit = wanted[:, None] == jnp.arange(ROWS)[None, :]
-    return jnp.stack([hit & (which == i)[:, None] for i in range(2)]).astype(BF)
+    hit = (col * (EP * STRIP) + src * STRIP + slot)[:, None] == np.arange(ROWS)[None, :]
+    return jnp.asarray(np.stack([hit & (which == i)[:, None] for i in range(2)]), dtype=BF)
 
 
 def solution(mesh):
     def device_body(x, grad_y, w_router, w_gate, w_up, w_down, ws_gate, ws_up, ws_down, topk_idx):
         tp = lax.axis_index('tp')
-        ep = lax.axis_index('ep')
-        per = LOCAL // TP
         ids = jnp.arange(EXPERTS, dtype=jnp.int32)
         hit = jnp.any(topk_idx[:, :, None] == ids[None, None, :], axis=1)
         before = jnp.tril(jnp.ones((TOK, TOK), BF), -1)
         rank = dot(before, hit.astype(BF))
         rank = jnp.where(hit, rank, -1.0).astype(jnp.int32)
         slot_hit = rank[:, :, None] == jnp.arange(STRIP, dtype=jnp.int32)[None, None, :]
-        token = jnp.arange(TOK, dtype=jnp.int32)[:, None, None] + 1
-        table = jnp.sum(jnp.where(slot_hit, token, 0), axis=0, dtype=jnp.int32) - 1
-        table = jnp.concatenate([table.reshape(EP, LOCAL * STRIP), jnp.zeros((8 - EP, LOCAL * STRIP), jnp.int32)], axis=0)
-        rows_near, tables, w_early, all_rows = gather_rows(jnp.concatenate([x, grad_y], axis=0), table, w_down)
-        mine = lax.dynamic_index_in_dim(tables, ep, 1, keepdims=False).reshape(EP, TP, LOCAL, STRIP)
-        w_late = []
-        for m in range(1, TP):
-            away = lax.dynamic_slice_in_dim(w_down, (tp ^ m) * per + EARLY, per - EARLY, axis=0)
-            w_late.append(lax.ppermute(away, 'tp', [(s, s ^ m) for s in range(TP)]))
-        base = (TOK * jnp.arange(EP, dtype=jnp.int32))[:, None, None, None]
-        slots = jnp.where(mine >= 0, mine + base, -1).transpose(1, 2, 0, 3).reshape(TP, LOCAL * EP * STRIP, 1)
-
-        *parts, h, dab, xe, de = main_call(jnp.stack([ep, tp]), rows_near, slots, w_router, ws_gate, ws_up, ws_down, permutations(tp), w_gate, w_up, w_down)
-        h_in = []
-        for m in range(1, TP):
-            away = lax.dynamic_slice_in_dim(h, (tp ^ m) * per, per, axis=0)
-            h_in.append(lax.ppermute(away, 'tp', [(s, s ^ m) for s in range(TP)]))
+        *parts, h, dab, xe, de, w_in, all_rows, h_in = main_call(
+            x, grad_y, topk_idx.T, w_router.T, ws_gate, ws_up, ws_down, permutations(), w_gate, w_up, w_down)
         firsts = [lax.ppermute(parts[2 * c + 1], 'tp', [(s, s ^ (2 - c)) for s in range(TP)]) for c in range(CHUNKS)]
-        o_send = out_call(tp.reshape(1), h, h_in, w_down, w_early, w_late)
+        o_send = out_call(tp.reshape(1), h, h_in, w_down, w_in)
 
         d_w_gate, d_w_up, d_w_down = grad_call(xe, de, h, dab)
 
@@ -578,7 +572,7 @@
         mark = slot_hit.reshape(TOK, EXPERTS * STRIP).astype(F32)
         mark16 = slot_hit[:, :, :CAP].reshape(TOK, EP, CHUNKS, PER_CHUNK, 2 * CAP).transpose(0, 1, 3, 2, 4)
         mark16 = jnp.pad(mark16, ((0, 0),) * 4 + ((0, 16 - 2 * CAP),)).reshape(TOK, EP * STEPS * 16).astype(BF)
-        y_out, dx_out, d_router = finish_call(parts[0::2], firsts, o_send, x, grad_y, w_router, mark, mark16, all_rows)
+        y_out, dx_out, d_router = finish_call(parts[0::2], firsts, o_send, x, grad_y, w_router.T, mark, mark16, all_rows)
         d_router = d_router.T
         return y_out, dx_out, d_router, d_w_gate, d_w_up, d_w_down, ds_gate, ds_up, ds_down
 

time: 303 us -> 251 us (0.83)
  waiting for transfers between devices: 71 us -> 32.4 us
  local copies, waits for them, and re-layouts: 21.2 us -> 13.3 us
  starting transfers between devices: 9.01 us -> 2.08 us
  Pallas kernels: 181 us -> 186 us
    ppermute x6 -> x0, waiting for transfers between devices: 70.9 us -> none  [the longest x3 70.9 us: device_body(): w_late.append(lax.ppermute(away, 'tp', [(s, s ^ m) for s in range(TP)]))]
    ppermute x2, waiting for transfers between devices: 0.01 us -> 32.4 us  [device_body(): lax.ppermute(parts[2 * c + 1], 'tp', [(s, s ^ 2 - c) for s in range(TP)])]
    ppermute x6 -> x0, starting transfers between devices: 7.01 us -> none  [the longest x3 3.52 us: device_body(): w_late.append(lax.ppermute(away, 'tp', [(s, s ^ m) for s in range(TP)]))]
    unnamed x52 -> x43, local copies, waits for them, and re-layouts: 11.2 us -> 4.5 us
    pallas_call x2 -> x1, Pallas kernels: 93.2 us -> 99.3 us  [main_call(): pl.pallas_call(main_kernel, name='main_call', grid=(STEPS,), in_specs=[vm...]
    dynamic_slice x3 -> x0, local copies, waits for them, and re-layouts: 3.84 us -> none  [the longest x1 3.06 us: device_body(): lax.dynamic_slice_in_dim(w_down, (tp ^ m) * per + EARLY, per - EARLY, axi...]
  transfers between devices with their start and end apart: 8 -> 2, of which waited for: 3 -> 2; matrix products, arithmetic and copies ran while one was open for 8% -> 10% of each run, Pallas kernels for 6% -> 7%
where the time goes in v3:
time: 251 us
  Pallas kernels  186 us (74%)
  waiting for transfers between devices  32.4 us (13%)
  matrix products  13.9 us (6%)
  local copies, waits for them, and re-layouts  13.3 us (5%)
    pallas_call x1, Pallas kernels, main_call(): pl.pallas_call(main_kernel, name='main_call', grid=(STEPS,), in_specs=[vm...  99.3 us
    pallas_call x1, Pallas kernels, finish_call(): pl.pallas_call(finish_kernel, name='finish_call', out_shape=(jax.ShapeDty...  69.6 us
    ppermute x2, waiting for transfers between devices, device_body(): lax.ppermute(parts[2 * c + 1], 'tp', [(s, s ^ 2 - c) for s in range(TP)])  32.4 us
    pallas_call x1, Pallas kernels, grad_call(): pl.pallas_call(grad_kernel, name='grad_call', grid=(LOCAL,), in_specs=[on...  15.6 us
    dot_general x3, matrix products, dot_tn(): lax.dot_general(a, b, (((0,), (0,)), ((), ())), preferred_element_type=F32)  6.82 us
    slice x1, local copies, waits for them, and re-layouts, device_body(): gy_all = all_rows[:, TOK:].reshape(NDEV * TOK, D)  5.17 us
  transfers between devices with their start and end apart: 2, of which 2 were waited for; matrix products, arithmetic and copies ran while one was open for 10% of the time, Pallas kernels for 7%

profile of v3, /device:TPU:0, one launch (start us, length us, event | category | flops | bytes accessed | tf_op | source)
XLA Modules:
  0.0 250.7 jit_solution(9179786799445297100)
XLA Ops:
  0.7 99.3 %main_call.1 = (f32[2,288,1536]{2,1,0:T(8,128)}, f32[2,288,1536]{2,1,0:T(8,128)}, f32[2,288,1536]{2,1,0:T(8,128)}, f32[2,288,1536]{2,1,0:T(8,128)}, bf16[16,128,...) custom-call(bf16[64,1536]{1,0:T(8,128)(2,1)} %x_ref.3, ...), custom_call_target="tpu_custom_call" | custom-call | flops 60000002048 | bytes 60000000 | tf_op jit(solution)/shard_map/main_call/pallas_call | solution.py:306
  100.0 1.5 collective-permute-start
  101.5 0.5 collective-permute-start.1
  102.6 5.2 %fusion.28 = (bf16[16,64,1536]{2,1,0:T(8,128)(2,1)}, bf16[16,64,1536]{2,1,0:T(8,128)(2,1)S(1)}) fusion(bf16[16,128,1536]{2,1,0:T(8,128)(2,1)} %get-tuple-element.33.all_hbm), kind=kLoop, calls=%fused_computation.41 | loop fusion | bytes 12582912 | tf_op jit(solution)/shard_map/slice | solution.py:563
  107.8 1.8 convolution_convert_fusion
  109.5 1.8 convolution_convert_fusion.1
  111.4 0.7 pad_convert_fusion
  112.2 1.6 copy.28
  113.7 1.0 copy.29.mark16_ref
  114.7 0.8 copy.27
  115.5 1.1 compare_convert_fusion.mark_ref
  116.6 3.3 %convolution_convert_fusion.2 = bf16[1024,256]{1,0:T(8,128)(2,1)S(1)} fusion(bf16[1024,1536]{1,0:T(8,128)(2,1)} %bitcast.37, bf16[256,1536]{1,0:T(8,128)(2,1)} %wsd_ref.1), kind=kOutput, calls=%fused_computation.8 | convolution fusion | flops 805568512 | bytes 4456448 | tf_op jit(solution)/shard_map/dot_general | solution.py:52
  120.0 2.2 fusion.12
  123.1 1.7 out_call.1.o_ref
  124.8 2.3 fusion.14
  127.1 2.3 fusion.10
  129.8 1.0 slice-done.7
  131.0 15.6 %grad_call.1 = (f32[16,1536,128]{2,1,0:T(8,128)}, f32[16,1536,128]{2,1,0:T(8,128)}, f32[16,128,1536]{2,1,0:T(8,128)}) custom-call(bf16[16,128,1536]{2,1,0:T(8,128)(2,1)S(1)} %bitcast.30, bf16[16,128,1536]{2,1,0:T(8,128)(2,1)S(1)} %bitcast.32, bf16[16,128,128]{2,1,0:T(8,128)(2,1)S(1)} %copy-done.1, bf16[16,128,256]{2,1,0:T(8,128)(2,1)S(1)} %copy-done.5), custom_call_target="tpu_custom_call" | custom-call | flops 10000000000 | bytes 55000000 | tf_op jit(solution)/shard_map/grad_call/pallas_call | solution.py:344
  146.6 31.2 %collective-permute-done.first0 = f32[2,288,1536]{2,1,0:T(8,128)} collective-permute-done((f32[2,288,1536]{2,1,0:T(8,128)}, f32[2,288,1536]{2,1,0:T(8,128)}, u32[]{:S(2)}, u32[]{:S(2)}) %collective-permute-start) | collective-permute-done | bytes 3538976 | tf_op jit(solution)/shard_map/ppermute | solution.py:557
  177.8 1.2 collective-permute-done.1.first1
  179.0 69.6 %finish_call.1 = (bf16[64,1536]{1,0:T(8,128)(2,1)S(1)}, bf16[64,1536]{1,0:T(8,128)(2,1)S(1)}, f32[64,1536]{1,0:T(8,128)S(1)}) custom-call(f32[2,288,1536]{2,1,0:T(8,128)} %get-tuple-element.26.keep0, f32[2,288,1536]{2,1,0:T(8,128)} %get-tuple-element.27.keep1, f32[2,288,1536]{2,1,0:T(8,128)} %collective-permute-done.first0, ...), custom_call_target="tpu_custom_call" | custom-call | flops 49999998976 | bytes 20000000 | tf_op jit(solution)/shard_map/finish_call/pallas_call | solution.py:522
  248.6 0.7 copy.33
  249.2 0.7 copy.34
  249.9 0.7 copy.35
  (52 shorter events, 2.1 us)
Async XLA Ops:
  0.6 101.4 %copy-start.7 = (s32[64,6]{0,1:T(8,128)S(1)}, s32[64,6]{0,1:T(8,128)}, u32[]{:S(2)}) copy-start(s32[64,6]{0,1:T(8,128)} %param.20) | copy-start | bytes 4612
  100.0 77.8 %collective-permute-start = (f32[2,288,1536]{2,1,0:T(8,128)}, f32[2,288,1536]{2,1,0:T(8,128)}, u32[]{:S(2)}, u32[]{:S(2)}) collective-permute-start(f32[2,288,1536]{2,1,0:T(8,128)} %get-tuple-element.28), channel_id=1, source_target_pairs={{0,8},{4,12},{8,0},{12,4},{1,9},{5,13},{9,1},{13,5},{2,10},{6,14},... | collective-permute-start | bytes 10616840 | tf_op jit(solution)/shard_map/ppermute | solution.py:557
  101.5 77.4 %collective-permute-start.1 = (f32[2,288,1536]{2,1,0:T(8,128)}, f32[2,288,1536]{2,1,0:T(8,128)}, u32[]{:S(2)}, u32[]{:S(2)}) collective-permute-start(f32[2,288,1536]{2,1,0:T(8,128)} %get-tuple-element.29), channel_id=1, source_target_pairs={{0,4},{4,0},{8,12},{12,8},{1,5},{5,1},{9,13},{13,9},{2,6},{6,2},{1... | collective-permute-start | bytes 10616840 | tf_op jit(solution)/shard_map/ppermute | solution.py:557
  102.6 5.2 %copy-start.8 = (bf16[1536,256]{1,0:T(8,128)(2,1)S(1)}, bf16[1536,256]{1,0:T(8,128)(2,1)}, u32[]{:S(2)}) copy-start(bf16[1536,256]{1,0:T(8,128)(2,1)} %wsg_ref.1) | copy-start | bytes 2359300
  107.8 1.8 copy-start.9
  115.5 4.4 %copy-start.6 = (bf16[16,64,1536]{2,1,0:T(8,128)(2,1)S(1)}, bf16[16,64,1536]{2,1,0:T(8,128)(2,1)}, u32[]{:S(2)}) copy-start(bf16[16,64,1536]{2,1,0:T(8,128)(2,1)} %get-tuple-element.43) | copy-start | bytes 9437188
  115.5 4.5 %copy-start.10 = (bf16[1024,256]{1,0:T(8,128)(2,1)S(1)}, bf16[1024,256]{1,0:T(8,128)(2,1)}, u32[]{:S(2)}) copy-start(bf16[1024,256]{1,0:T(8,128)(2,1)} %convolution_convert_fusion) | copy-start | bytes 1572868
  115.5 4.5 %copy-start.11 = (bf16[1024,256]{1,0:T(8,128)(2,1)S(1)}, bf16[1024,256]{1,0:T(8,128)(2,1)}, u32[]{:S(2)}) copy-start(bf16[1024,256]{1,0:T(8,128)(2,1)} %convolution_convert_fusion.1) | copy-start | bytes 1572868
  116.6 5.6 %slice-start = ((s8[4718592]{0:T(1024)(128)(4,1)}), s8[4194304]{0:T(1024)(128)(4,1)S(1)}, s32[]{:S(2)}) async-start(s8[4718592]{0:T(1024)(128)(4,1)} %bitcast.22), calls=%async_computation | async-start | bytes 8388608
  116.6 5.6 %slice-start.2 = ((s8[6291456]{0:T(1024)(128)(4,1)}), s8[4194304]{0:T(1024)(128)(4,1)S(1)}, s32[]{:S(2)}) async-start(s8[6291456]{0:T(1024)(128)(4,1)} %bitcast.24), calls=%async_computation.2 | async-start | bytes 8388608
  120.0 2.2 slice-start.1
  120.0 2.5 %slice-start.3 = ((s8[6291456]{0:T(1024)(128)(4,1)}), s8[2097152]{0:T(1024)(128)(4,1)S(1)}, s32[]{:S(2)}) async-start(s8[6291456]{0:T(1024)(128)(4,1)} %bitcast.24), calls=%async_computation.3 | async-start | bytes 4194304
  120.0 2.8 %copy-start = (bf16[3,4,128,128]{3,2,1,0:T(8,128)(2,1)S(1)}, bf16[3,4,128,128]{3,2,1,0:T(8,128)(2,1)}, u32[]{:S(2)}) copy-start(bf16[3,4,128,128]{3,2,1,0:T(8,128)(2,1)} %get-tuple-element.31.h1.h2.h3) | copy-start | bytes 1179652
  120.0 3.1 %copy-start.1 = (bf16[16,128,128]{2,1,0:T(8,128)(2,1)S(1)}, bf16[16,128,128]{2,1,0:T(8,128)(2,1)}, u32[]{:S(2)}) copy-start(bf16[16,128,128]{2,1,0:T(8,128)(2,1)} %get-tuple-element.30.h0.h_ref) | copy-start | bytes 1572868
  124.8 4.7 %slice-start.4 = ((s8[6291456]{0:T(1024)(128)(4,1)}), s8[4194304]{0:T(1024)(128)(4,1)S(1)}, s32[]{:S(2)}) async-start(s8[6291456]{0:T(1024)(128)(4,1)} %bitcast.29), calls=%async_computation.4 | async-start | bytes 8388608
  124.8 4.7 %slice-start.6 = ((s8[6291456]{0:T(1024)(128)(4,1)}), s8[4194304]{0:T(1024)(128)(4,1)S(1)}, s32[]{:S(2)}) async-start(s8[6291456]{0:T(1024)(128)(4,1)} %bitcast.31), calls=%async_computation.6 | async-start | bytes 8388608
  127.1 2.6 %slice-start.5 = ((s8[6291456]{0:T(1024)(128)(4,1)}), s8[2097152]{0:T(1024)(128)(4,1)S(1)}, s32[]{:S(2)}) async-start(s8[6291456]{0:T(1024)(128)(4,1)} %bitcast.29), calls=%async_computation.5 | async-start | bytes 4194304
  127.1 3.6 %slice-start.7 = ((s8[6291456]{0:T(1024)(128)(4,1)}), s8[2097152]{0:T(1024)(128)(4,1)S(1)}, s32[]{:S(2)}) async-start(s8[6291456]{0:T(1024)(128)(4,1)} %bitcast.31), calls=%async_computation.7 | async-start | bytes 4194304
  127.1 3.8 %copy-start.5 = (bf16[16,128,256]{2,1,0:T(8,128)(2,1)S(1)}, bf16[16,128,256]{2,1,0:T(8,128)(2,1)}, u32[]{:S(2)}) copy-start(bf16[16,128,256]{2,1,0:T(8,128)(2,1)} %get-tuple-element.39.dab_ref) | copy-start | bytes 3145732
  130.9 48.0 %copy-start.2 = (bf16[64,1536]{1,0:T(8,128)(2,1)S(1)}, bf16[64,1536]{1,0:T(8,128)(2,1)}, u32[]{:S(2)}) copy-start(bf16[64,1536]{1,0:T(8,128)(2,1)} %x_ref.3) | copy-start | bytes 589828
  131.0 48.0 %copy-start.3 = (bf16[64,1536]{1,0:T(8,128)(2,1)S(1)}, bf16[64,1536]{1,0:T(8,128)(2,1)}, u32[]{:S(2)}) copy-start(bf16[64,1536]{1,0:T(8,128)(2,1)} %gy_ref.3) | copy-start | bytes 589828
  131.0 48.0 %copy-start.4 = (bf16[1536,64]{0,1:T(8,128)(2,1)S(1)}, bf16[1536,64]{0,1:T(8,128)(2,1)}, u32[]{:S(2)}) copy-start(bf16[1536,64]{0,1:T(8,128)(2,1)} %param.13) | copy-start | bytes 589828

commit v4 on v3

--- a/solution.py
+++ b/solution.py
@@ -29,6 +29,7 @@
 BLK = PAIR_ROWS + SH_ROWS
 CHUNKS = 2
 PER_CHUNK = STEPS // CHUNKS
+PARTS = 4
 
 BIT_Y, BIT_Z, BIT_C, BIT_X = 1, 2, 4, 8
 
@@ -69,7 +70,7 @@
     tp = lax.axis_index('tp')
     ep = lax.axis_index('ep')
     me = ep * TP + tp
-    third = D // 3
+    width = D // PARTS
 
     def peer(mask):
         return (flip_mask(tp, mask & 3), flip_mask(ep, mask >> 2))
@@ -86,12 +87,12 @@
     for c in own:
         c.wait()
 
-    orders = [(BIT_Y, BIT_Z, BIT_X), (BIT_Z, BIT_Y, BIT_X), (BIT_Y, BIT_Z, BIT_X), (BIT_Z, BIT_Y, BIT_X)]
+    orders = [(BIT_Y, BIT_Z, BIT_X) if part % 2 == 0 else (BIT_Z, BIT_Y, BIT_X) for part in range(PARTS + 1)]
 
     def view(part, block):
-        if part == 3:
+        if part == PARTS:
             return tabs_ref.at[block]
-        return all_ref.at[block, :, pl.ds(part * third, third)]
+        return all_ref.at[block, :, pl.ds(part * width, width)]
 
     sent = []
 
@@ -111,7 +112,7 @@
             send_sem=send_sem.at[part, k], recv_sem=recv_sem.at[part, k],
             device_id=peer(BIT_C), device_id_type=MESH).wait_recv()
 
-    parts = (3, 0, 1, 2)
+    parts = (PARTS,) + tuple(range(PARTS))
     for step in range(3):
         for part in parts:
             send(part, 0, orders[part][step])
@@ -170,10 +171,10 @@
     return ((0, 1), (2, 3)) if chunk % 2 == 0 else ((0, 2), (1, 3))
 
 
-def main_kernel(x_ref, gy_ref, tab_ref, w_all_ref, wr_ref, wsg_ref, wsu_ref, wsd_ref, perm_ref, wg_ref, wu_ref, wd_ref, *refs):
+def main_kernel(x_ref, gy_ref, tab_ref, w_all_ref, wr_hbm, wsg_hbm, wsu_hbm, wsd_hbm, perm_ref, wg_ref, wu_ref, wd_ref, *refs):
     chunk_refs, refs = refs[:2 * CHUNKS], refs[2 * CHUNKS:]
     (h_ref, dab_ref, xe_hbm, de_hbm, w_in_ref, keep_ref, h_in_ref, all_ref, tabs_ref, xe, de, sh, hs, sems,
-     send_sem, recv_sem, local_sem, w_send, w_recv, keep_sem, h_send, h_recv) = refs
+     send_sem, recv_sem, local_sem, w_send, w_recv, keep_sem, h_send, h_recv, wr_ref, wsg_ref, wsu_ref, wsd_ref, late_sem) = refs
     step = pl.program_id(0)
     g = lax.axis_index('ep')
     tp = lax.axis_index('tp')
@@ -184,7 +185,13 @@
 
     @pl.when(step == 0)
     def _():
+        late_copies = [pltpu.make_async_copy(src, dst, late_sem.at[n]) for n, (src, dst) in enumerate((
+            (wr_hbm, wr_ref), (wsg_hbm, wsg_ref), (wsu_hbm, wsu_ref), (wsd_hbm, wsd_ref)))]
+        for c in late_copies:
+            c.start()
         gather_rows(x_ref, gy_ref, tab_ref, w_all_ref, all_ref, tabs_ref, w_in_ref, keep_ref, send_sem, recv_sem, local_sem, w_send, w_recv, keep_sem)
+        for c in late_copies:
+            c.wait()
         n_rows = LOCAL * EP * STRIP
         expert = g * LOCAL + lax.broadcasted_iota(jnp.int32, (LOCAL, TOK), 0)
         early = lax.broadcasted_iota(jnp.int32, (EP * TOK, EP * TOK), 0)
@@ -299,7 +306,6 @@
         return pl.BlockSpec((2,) + a.shape[1:], lambda i: (i, 0, 0))
 
     hbm = pl.BlockSpec(memory_space=pltpu.HBM)
-    vmem = pl.BlockSpec(memory_space=pltpu.VMEM)
     dma = pltpu.SemaphoreType.DMA
     chunk_specs = [pl.BlockSpec((2, BLK, D), lambda i, c=n // 2: (0, jnp.clip(i - PER_CHUNK * c, 0, PER_CHUNK - 1), 0))
                    for n in range(2 * CHUNKS)]
@@ -307,7 +313,7 @@
         main_kernel,
         name='main_call',
         grid=(STEPS,),
-        in_specs=[vmem, vmem, vmem, hbm, whole(w_router), whole(ws_gate), whole(ws_up), whole(ws_down), whole(perm),
+        in_specs=[hbm] * 8 + [whole(perm),
                   pair(w_gate), pair(w_up), pair(w_down)],
         out_specs=chunk_specs + [
             pl.BlockSpec((2, ROWS, width), lambda i: (i, 0, 0)),
@@ -315,7 +321,8 @@
         scratch_shapes=[pltpu.VMEM((NDEV, 2 * TOK, D), BF), pltpu.VMEM((NDEV,) + table.shape, jnp.int32),
                         pltpu.VMEM((LOCAL, ROWS, D), BF), pltpu.VMEM((LOCAL, ROWS, D), BF),
                         pltpu.VMEM((2, TP, TOK, D), F32), pltpu.VMEM((LOCAL, ROWS, width), BF), dma((2,)),
-                        dma((4, 16)), dma((4, 16)), dma((3,)), dma((TP - 1,)), dma((TP - 1,)), dma((NDEV,)), dma((TP - 1,)), dma((TP - 1,))],
+                        dma((PARTS + 1, 16)), dma((PARTS + 1, 16)), dma((3,)), dma((TP - 1,)), dma((TP - 1,)), dma((NDEV,)), dma((TP - 1,)), dma((TP - 1,)),
+                        pltpu.VMEM(w_router.shape, BF), pltpu.VMEM(ws_gate.shape, BF), pltpu.VMEM(ws_up.shape, BF), pltpu.VMEM(ws_down.shape, BF), dma((4,))],
         out_shape=[jax.ShapeDtypeStruct((2, BLK * PER_CHUNK, D), F32)] * (2 * CHUNKS) + [
             jax.ShapeDtypeStruct((LOCAL, ROWS, width), BF),
             jax.ShapeDtypeStruct((LOCAL, ROWS, 2 * width), BF),
@@ -441,7 +448,11 @@
         loads[n][0].wait()
         loads[n][1].wait()
         snd[n] = k1[n] + f1[n]
-        send(snd.at[n], rcv.at[n], (s2_send, s2_recv), n, (BIT_Y, BIT_Z)[pieces[n][0]])
+        pass_rows(n, 0)
+
+    def pass_rows(n, which):
+        rows = (pl.ds(0, PAIR_ROWS), pl.ds(PAIR_ROWS, SH_ROWS))[which]
+        send(snd.at[n, rows], rcv.at[n, rows], (s2_send, s2_recv), (n, which), (BIT_Y, BIT_Z)[pieces[n][0]])
 
     for n in range(4):
         second_stage(n)
@@ -468,31 +479,41 @@
     d_scores = GATE_SCALE * (dot_nt(hi, spread) + dot_nt(mid, spread) + dot_nt(low, spread))
     d_logits = probs * (d_scores - jnp.sum(probs * d_scores, axis=-1, keepdims=True))
     dl[me] = jnp.concatenate([d_logits[:TOK // 2], d_logits[TOK // 2:]], axis=1)
-    for mask in range(1, NDEV):
-        send(dl.at[me], dl.at[me], (dl_send, dl_recv), mask, mask)
+    columns, copies = (BIT_Y, BIT_Z, BIT_Y | BIT_Z), (BIT_X, BIT_C, BIT_X | BIT_C)
+
+    def pass_dl(k, mask):
+        block = dl.at[flip_mask(me, k)]
+        send(block, block, (dl_send, dl_recv), k ^ mask, mask)
+
+    for mask in columns + copies:
+        pass_dl(0, mask)
     for n in range(4, len(pieces)):
         second_stage(n)
+    for n in range(len(pieces)):
+        pass_rows(n, 1)
     hi, mid, low = split3(d_logits)
     dx_router = dot(hi, wr) + dot(mid, wr) + dot(low, wr)
 
     def finish_piece(n):
-        c, i = pieces[n]
-        arrived(rcv.at[n], (s2_send, s2_recv), n)
+        arrived(rcv.at[n, pl.ds(0, PAIR_ROWS)], (s2_send, s2_recv), (n, 0))
         loads[n][2].wait()
         loads[n][3].wait()
-        own = k0[n] + f0[n] + rcv[n]
+        own = k0[n, :PAIR_ROWS] + f0[n, :PAIR_ROWS] + rcv[n, :PAIR_ROWS]
         for s in range(EP):
             rows = own[2 * CAP * s:2 * CAP * (s + 1)]
             ret[s, n] = jnp.concatenate([rows, jnp.zeros((16 - 2 * CAP, D), F32)], axis=0).astype(BF)
         for at, mask in enumerate((BIT_X, BIT_C, BIT_X | BIT_C)):
             send(ret.at[flip_mask(ep, mask >> 2), n], ret_in.at[ep, n], (ret_send, ret_recv), (n, at), mask)
         ret_in[ep, n] = ret[ep, n]
-        (s_rows, d_rows)[c][SH_ROWS * i:SH_ROWS * (i + 1), :] = own[PAIR_ROWS:]
 
     for n in range(4):
         finish_piece(n)
-    for mask in range(1, NDEV):
-        arrived(dl.at[flip_mask(me, mask)], (dl_send, dl_recv), mask)
+    for k in columns:
+        arrived(dl.at[flip_mask(me, k)], (dl_send, dl_recv), k)
+        for mask in copies:
+            pass_dl(k, mask)
+    for k in range(TP, NDEV):
+        arrived(dl.at[flip_mask(me, k)], (dl_send, dl_recv), k)
     x_load.wait()
     total = jnp.zeros((EXPERTS, D), F32)
     for half in range(2):
@@ -502,6 +523,9 @@
     drt_ref[...] = total
     for n in range(4, len(pieces)):
         finish_piece(n)
+    for n, (c, i) in enumerate(pieces):
+        arrived(rcv.at[n, pl.ds(PAIR_ROWS, SH_ROWS)], (s2_send, s2_recv), (n, 1))
+        (s_rows, d_rows)[c][SH_ROWS * i:SH_ROWS * (i + 1), :] = k0[n, PAIR_ROWS:] + f0[n, PAIR_ROWS:] + rcv[n, PAIR_ROWS:]
     y_ref[...] = (s_rows[...] + routed).astype(BF)
     for n in range(len(pieces)):
         for at, mask in enumerate((BIT_X, BIT_C, BIT_X | BIT_C)):
@@ -527,7 +551,7 @@
         out_specs=(vmem, vmem, vmem),
         scratch_shapes=[piece] * 6 + [ret, ret, pltpu.VMEM((NDEV, LOCAL // TP * STRIP, D), BF), pltpu.VMEM((NDEV, TOK // 2, 2 * EXPERTS), F32),
                                       pltpu.VMEM((NDEV, TOK, D), BF), pltpu.VMEM((TOK, D), F32), pltpu.VMEM((TOK, D), F32),
-                                      dma((4, pieces)), dma, dma((pieces,)), dma((pieces,)), dma((pieces, 3)), dma((pieces, 3)),
+                                      dma((4, pieces)), dma, dma((pieces, 2)), dma((pieces, 2)), dma((pieces, 3)), dma((pieces, 3)),
                                       dma((NDEV,)), dma((NDEV,)), dma((NDEV,)), dma((NDEV,)), dma],
         compiler_params=pltpu.CompilerParams(collective_id=1, has_side_effects=True, vmem_limit_bytes=48 << 20),
         cost_estimate=pl.CostEstimate(flops=50_000_000_000, bytes_accessed=20_000_000, transcendentals=0),

time: 251 us -> 244 us (0.972)
  Pallas kernels: 186 us -> 180 us
    pallas_call x1, Pallas kernels: 69.6 us -> 64.4 us  [finish_call(): pl.pallas_call(finish_kernel, name='finish_call', out_shape=(jax.ShapeDty...]
where the time goes in v4:
time: 244 us
  Pallas kernels  180 us (74%)
  waiting for transfers between devices  32.1 us (13%)
  matrix products  13.9 us (6%)
  local copies, waits for them, and re-layouts  13.3 us (5%)
    pallas_call x1, Pallas kernels, main_call(): pl.pallas_call(main_kernel, name='main_call', grid=(STEPS,), in_specs=[hb...  98.3 us
    pallas_call x1, Pallas kernels, finish_call(): pl.pallas_call(finish_kernel, name='finish_call', out_shape=(jax.ShapeDty...  64.4 us
    ppermute x2, waiting for transfers between devices, device_body(): lax.ppermute(parts[2 * c + 1], 'tp', [(s, s ^ 2 - c) for s in range(TP)])  32.1 us
    pallas_call x1, Pallas kernels, grad_call(): pl.pallas_call(grad_kernel, name='grad_call', grid=(LOCAL,), in_specs=[on...  15.6 us
    dot_general x3, matrix products, dot_tn(): lax.dot_general(a, b, (((0,), (0,)), ((), ())), preferred_element_type=F32)  6.82 us
    slice x1, local copies, waits for them, and re-layouts, device_body(): gy_all = all_rows[:, TOK:].reshape(NDEV * TOK, D)  5.17 us
  transfers between devices with their start and end apart: 2, of which 2 were waited for; matrix products, arithmetic and copies ran while one was open for 10% of the time, Pallas kernels for 7%

profile of v4, /device:TPU:0, one launch (start us, length us, event | category | flops | bytes accessed | tf_op | source)
XLA Modules:
  0.0 243.7 jit_solution(14410452939914811577)
XLA Ops:
  0.7 98.3 %main_call.1 = (f32[2,288,1536]{2,1,0:T(8,128)}, f32[2,288,1536]{2,1,0:T(8,128)}, f32[2,288,1536]{2,1,0:T(8,128)}, f32[2,288,1536]{2,1,0:T(8,128)}, bf16[16,128,...) custom-call(bf16[64,1536]{1,0:T(8,128)(2,1)} %x_ref.3, ...), custom_call_target="tpu_custom_call" | custom-call | flops 60000002048 | bytes 60000000 | tf_op jit(solution)/shard_map/main_call/pallas_call | solution.py:312
  98.9 0.5 collective-permute-start
  99.4 1.1 collective-permute-start.1
  101.1 5.2 %fusion.28 = (bf16[16,64,1536]{2,1,0:T(8,128)(2,1)}, bf16[16,64,1536]{2,1,0:T(8,128)(2,1)S(1)}) fusion(bf16[16,128,1536]{2,1,0:T(8,128)(2,1)} %get-tuple-element.33.all_hbm), kind=kLoop, calls=%fused_computation.41 | loop fusion | bytes 12582912 | tf_op jit(solution)/shard_map/slice | solution.py:587
  106.2 1.8 convolution_convert_fusion
  108.0 1.8 convolution_convert_fusion.1
  109.9 0.7 pad_convert_fusion
  110.7 1.6 copy.28
  112.2 1.0 copy.29.mark16_ref
  113.2 0.8 copy.27
  114.0 1.1 compare_convert_fusion.mark_ref
  115.1 3.3 %convolution_convert_fusion.2 = bf16[1024,256]{1,0:T(8,128)(2,1)S(1)} fusion(bf16[1024,1536]{1,0:T(8,128)(2,1)} %bitcast.37, bf16[256,1536]{1,0:T(8,128)(2,1)} %wsd_hbm.1), kind=kOutput, calls=%fused_computation.8 | convolution fusion | flops 805568512 | bytes 4456448 | tf_op jit(solution)/shard_map/dot_general | solution.py:53
  118.5 2.2 fusion.12
  121.3 0.3 copy-done.1
  121.6 1.7 out_call.1.o_ref
  123.3 2.3 fusion.14
  125.6 2.3 fusion.10
  128.3 1.0 slice-done.7
  129.5 15.6 %grad_call.1 = (f32[16,1536,128]{2,1,0:T(8,128)}, f32[16,1536,128]{2,1,0:T(8,128)}, f32[16,128,1536]{2,1,0:T(8,128)}) custom-call(bf16[16,128,1536]{2,1,0:T(8,128)(2,1)S(1)} %bitcast.30, bf16[16,128,1536]{2,1,0:T(8,128)(2,1)S(1)} %bitcast.32, bf16[16,128,128]{2,1,0:T(8,128)(2,1)S(1)} %copy-done.1, bf16[16,128,256]{2,1,0:T(8,128)(2,1)S(1)} %copy-done.5), custom_call_target="tpu_custom_call" | custom-call | flops 10000000000 | bytes 55000000 | tf_op jit(solution)/shard_map/grad_call/pallas_call | solution.py:351
  145.1 31.9 %collective-permute-done.first0 = f32[2,288,1536]{2,1,0:T(8,128)} collective-permute-done((f32[2,288,1536]{2,1,0:T(8,128)}, f32[2,288,1536]{2,1,0:T(8,128)}, u32[]{:S(2)}, u32[]{:S(2)}) %collective-permute-start) | collective-permute-done | bytes 3538976 | tf_op jit(solution)/shard_map/ppermute | solution.py:581
  177.2 64.4 %finish_call.1 = (bf16[64,1536]{1,0:T(8,128)(2,1)S(1)}, bf16[64,1536]{1,0:T(8,128)(2,1)S(1)}, f32[64,1536]{1,0:T(8,128)S(1)}) custom-call(f32[2,288,1536]{2,1,0:T(8,128)} %get-tuple-element.26.keep0, f32[2,288,1536]{2,1,0:T(8,128)} %get-tuple-element.27.keep1, f32[2,288,1536]{2,1,0:T(8,128)} %collective-permute-done.first0, ...), custom_call_target="tpu_custom_call" | custom-call | flops 49999998976 | bytes 20000000 | tf_op jit(solution)/shard_map/finish_call/pallas_call | solution.py:546
  241.6 0.7 copy.33
  242.3 0.7 copy.34
  242.9 0.7 copy.35
  (52 shorter events, 1.9 us)
Async XLA Ops:
  0.6 99.9 %copy-start.7 = (s32[64,6]{0,1:T(8,128)S(1)}, s32[64,6]{0,1:T(8,128)}, u32[]{:S(2)}) copy-start(s32[64,6]{0,1:T(8,128)} %param.20) | copy-start | bytes 4612
  98.9 78.0 %collective-permute-start = (f32[2,288,1536]{2,1,0:T(8,128)}, f32[2,288,1536]{2,1,0:T(8,128)}, u32[]{:S(2)}, u32[]{:S(2)}) collective-permute-start(f32[2,288,1536]{2,1,0:T(8,128)} %get-tuple-element.28), channel_id=1, source_target_pairs={{0,8},{4,12},{8,0},{12,4},{1,9},{5,13},{9,1},{13,5},{2,10},{6,14},... | collective-permute-start | bytes 10616840 | tf_op jit(solution)/shard_map/ppermute | solution.py:581
  99.4 77.7 %collective-permute-start.1 = (f32[2,288,1536]{2,1,0:T(8,128)}, f32[2,288,1536]{2,1,0:T(8,128)}, u32[]{:S(2)}, u32[]{:S(2)}) collective-permute-start(f32[2,288,1536]{2,1,0:T(8,128)} %get-tuple-element.29), channel_id=1, source_target_pairs={{0,4},{4,0},{8,12},{12,8},{1,5},{5,1},{9,13},{13,9},{2,6},{6,2},{1... | collective-permute-start | bytes 10616840 | tf_op jit(solution)/shard_map/ppermute | solution.py:581
  101.0 5.2 %copy-start.8 = (bf16[1536,256]{1,0:T(8,128)(2,1)S(1)}, bf16[1536,256]{1,0:T(8,128)(2,1)}, u32[]{:S(2)}) copy-start(bf16[1536,256]{1,0:T(8,128)(2,1)} %wsg_hbm.1) | copy-start | bytes 2359300
  106.2 1.8 copy-start.9
  114.0 4.5 %copy-start.6 = (bf16[16,64,1536]{2,1,0:T(8,128)(2,1)S(1)}, bf16[16,64,1536]{2,1,0:T(8,128)(2,1)}, u32[]{:S(2)}) copy-start(bf16[16,64,1536]{2,1,0:T(8,128)(2,1)} %get-tuple-element.43) | copy-start | bytes 9437188
  114.0 4.5 %copy-start.10 = (bf16[1024,256]{1,0:T(8,128)(2,1)S(1)}, bf16[1024,256]{1,0:T(8,128)(2,1)}, u32[]{:S(2)}) copy-start(bf16[1024,256]{1,0:T(8,128)(2,1)} %convolution_convert_fusion) | copy-start | bytes 1572868
  114.0 4.5 %copy-start.11 = (bf16[1024,256]{1,0:T(8,128)(2,1)S(1)}, bf16[1024,256]{1,0:T(8,128)(2,1)}, u32[]{:S(2)}) copy-start(bf16[1024,256]{1,0:T(8,128)(2,1)} %convolution_convert_fusion.1) | copy-start | bytes 1572868
  115.1 5.6 %slice-start = ((s8[4718592]{0:T(1024)(128)(4,1)}), s8[4194304]{0:T(1024)(128)(4,1)S(1)}, s32[]{:S(2)}) async-start(s8[4718592]{0:T(1024)(128)(4,1)} %bitcast.22), calls=%async_computation | async-start | bytes 8388608
  115.1 5.6 %slice-start.2 = ((s8[6291456]{0:T(1024)(128)(4,1)}), s8[4194304]{0:T(1024)(128)(4,1)S(1)}, s32[]{:S(2)}) async-start(s8[6291456]{0:T(1024)(128)(4,1)} %bitcast.24), calls=%async_computation.2 | async-start | bytes 8388608
  118.5 2.2 slice-start.1
  118.5 2.5 %slice-start.3 = ((s8[6291456]{0:T(1024)(128)(4,1)}), s8[2097152]{0:T(1024)(128)(4,1)S(1)}, s32[]{:S(2)}) async-start(s8[6291456]{0:T(1024)(128)(4,1)} %bitcast.24), calls=%async_computation.3 | async-start | bytes 4194304
  118.5 2.7 %copy-start = (bf16[3,4,128,128]{3,2,1,0:T(8,128)(2,1)S(1)}, bf16[3,4,128,128]{3,2,1,0:T(8,128)(2,1)}, u32[]{:S(2)}) copy-start(bf16[3,4,128,128]{3,2,1,0:T(8,128)(2,1)} %get-tuple-element.31.h1.h2.h3) | copy-start | bytes 1179652
  118.5 3.1 %copy-start.1 = (bf16[16,128,128]{2,1,0:T(8,128)(2,1)S(1)}, bf16[16,128,128]{2,1,0:T(8,128)(2,1)}, u32[]{:S(2)}) copy-start(bf16[16,128,128]{2,1,0:T(8,128)(2,1)} %get-tuple-element.30.h0.h_ref) | copy-start | bytes 1572868
  123.3 4.7 %slice-start.4 = ((s8[6291456]{0:T(1024)(128)(4,1)}), s8[4194304]{0:T(1024)(128)(4,1)S(1)}, s32[]{:S(2)}) async-start(s8[6291456]{0:T(1024)(128)(4,1)} %bitcast.29), calls=%async_computation.4 | async-start | bytes 8388608
  123.3 4.7 %slice-start.6 = ((s8[6291456]{0:T(1024)(128)(4,1)}), s8[4194304]{0:T(1024)(128)(4,1)S(1)}, s32[]{:S(2)}) async-start(s8[6291456]{0:T(1024)(128)(4,1)} %bitcast.31), calls=%async_computation.6 | async-start | bytes 8388608
  125.6 2.6 %slice-start.5 = ((s8[6291456]{0:T(1024)(128)(4,1)}), s8[2097152]{0:T(1024)(128)(4,1)S(1)}, s32[]{:S(2)}) async-start(s8[6291456]{0:T(1024)(128)(4,1)} %bitcast.29), calls=%async_computation.5 | async-start | bytes 4194304
  125.6 3.6 %slice-start.7 = ((s8[6291456]{0:T(1024)(128)(4,1)}), s8[2097152]{0:T(1024)(128)(4,1)S(1)}, s32[]{:S(2)}) async-start(s8[6291456]{0:T(1024)(128)(4,1)} %bitcast.31), calls=%async_computation.7 | async-start | bytes 4194304
  125.6 3.8 %copy-start.5 = (bf16[16,128,256]{2,1,0:T(8,128)(2,1)S(1)}, bf16[16,128,256]{2,1,0:T(8,128)(2,1)}, u32[]{:S(2)}) copy-start(bf16[16,128,256]{2,1,0:T(8,128)(2,1)} %get-tuple-element.39.dab_ref) | copy-start | bytes 3145732
  129.4 47.7 %copy-start.2 = (bf16[64,1536]{1,0:T(8,128)(2,1)S(1)}, bf16[64,1536]{1,0:T(8,128)(2,1)}, u32[]{:S(2)}) copy-start(bf16[64,1536]{1,0:T(8,128)(2,1)} %x_ref.3) | copy-start | bytes 589828
  129.5 47.7 %copy-start.3 = (bf16[64,1536]{1,0:T(8,128)(2,1)S(1)}, bf16[64,1536]{1,0:T(8,128)(2,1)}, u32[]{:S(2)}) copy-start(bf16[64,1536]{1,0:T(8,128)(2,1)} %gy_ref.3) | copy-start | bytes 589828
  129.5 47.7 %copy-start.4 = (bf16[1536,64]{0,1:T(8,128)(2,1)S(1)}, bf16[1536,64]{0,1:T(8,128)(2,1)}, u32[]{:S(2)}) copy-start(bf16[1536,64]{0,1:T(8,128)(2,1)} %param.13) | copy-start | bytes 589828
